TPU v7x, 32 devices: a whole 2x2x4 slice. The times are simulated.
32 devices in a mesh: tm: 8 (over z, y), node: 4 (over x, core).
Axes of the slice: x: 2, y: 2, z: 4, core: 2. Of those that a mesh axis runs over, the one named last changes fastest.
Arguments:
- slice_starts: float32 [8, 32, 16384], P('tm'), may hold values from -1 to 1
- coupling: float32 [32, 16384], replicated, may hold values from 0.03 to 0.25
Outputs:
- node_values: float32 [8, 4, 32, 16384], P('tm', 'node')
- residual_log: float32 [3, 32], replicated
All inputs are finite; a program needn't handle non-finite values.
Results may differ from a plain program's by a relative error of at most 0.0001.
Values sent between devices are 32-bit elements.
No kernel may reach another device: no remote copies, remote signals or barrier semaphores. Data moves between devices by JAX's collectives and lax.ppermute only.
A program may use at most 128 MiB of HBM per device.

v0:
```python
import jax
import jax.numpy as jnp
from jax import lax
from jax.sharding import PartitionSpec as P

M = 4
SWEEPS = 3
NEWTON = 2


time_step = 0.5
log_floor = 0.05


def spread(value, axis, root):
    mine = lax.axis_index(axis) == root
    return lax.psum(jnp.where(mine, value, jnp.zeros_like(value)), axis)


def passed_along(value, axis, by):
    size = lax.axis_size(axis)
    pairs = [(i, i + by) for i in range(size) if 0 <= i + by < size]
    return lax.ppermute(value, axis, pairs)


def legendre_gap(point, node_count):
    before = 1.0
    current = point
    for degree in range(1, node_count):
        following = ((2 * degree + 1) * point * current - degree * before) / (degree + 1)
        before = current
        current = following
    return current - before


def collocation(node_count):
    points = []
    samples = 4000
    for sample_index in range(samples - 1):
        lower_end = -1.0 + 2.0 * sample_index / samples
        upper_end = -1.0 + 2.0 * (sample_index + 1) / samples
        lower_value = legendre_gap(lower_end, node_count)
        upper_value = legendre_gap(upper_end, node_count)
        if lower_value * upper_value < 0.0:
            for halving in range(80):
                middle = 0.5 * (lower_end + upper_end)
                middle_value = legendre_gap(middle, node_count)
                if lower_value * middle_value <= 0.0:
                    upper_end = middle
                else:
                    lower_end = middle
                    lower_value = middle_value
            points.append(0.5 * (lower_end + upper_end))
    points.append(1.0)
    node_times = [(point + 1.0) / 2.0 for point in points]
    matrix = [[0.0] * node_count for row_index in range(node_count)]
    for column in range(node_count):
        coeffs = [1.0]
        for other in range(node_count):
            if other != column:
                scale = node_times[column] - node_times[other]
                shifted = [0.0] + coeffs
                scaled = [value * node_times[other] for value in coeffs] + [0.0]
                coeffs = [(shifted[power] - scaled[power]) / scale for power in range(len(shifted))]
        for row_index in range(node_count):
            upper_time = node_times[row_index]
            matrix[row_index][column] = sum(
                (
                    coeffs[power] * upper_time ** (power + 1) / (power + 1)
                    for power in range(len(coeffs))
                )
            )
    return (node_times, matrix)


def operator_term(field_values, coupling):
    right_side = jnp.roll(field_values, -1, axis=-1)
    left_side = jnp.roll(field_values, 1, axis=-1)
    left_coupling = jnp.roll(coupling, 1, axis=-1)
    cubic = field_values * field_values * field_values
    return (
        coupling * (right_side - field_values)
        - left_coupling * (field_values - left_side)
        + field_values
        - cubic
    )


def body(slice_starts, coupling):
    node_times, matrix = collocation(M)
    weights = jnp.asarray(matrix, jnp.float32)
    diag_weights = jnp.asarray([time_step * moment / M for moment in node_times], jnp.float32)
    node_pos = lax.axis_index("node")
    slice_pos = lax.axis_index("tm")
    systems, cells = coupling.shape
    initial = slice_starts[0]
    implicit = diag_weights[node_pos]
    row_weights = weights[node_pos]
    node_state = initial
    totals = []
    for sweep_index in range(SWEEPS):
        if sweep_index == 0:
            end_value = initial
        else:
            end_value = spread(node_state, "node", M - 1)
        arrived = passed_along(end_value, "tm", 1)
        start_value = jnp.where(slice_pos == 0, initial, arrived)
        forcing = operator_term(node_state, coupling)
        segment = lax.all_gather(forcing, "node", axis=0, tiled=True)
        positions = jnp.arange(segment.shape[0], dtype=jnp.int32)
        owners = positions // systems
        members = positions % systems
        factors = jnp.sum(
            jnp.where(
                owners[:, None] == jnp.arange(M, dtype=jnp.int32)[None], row_weights[None], 0.0
            ),
            axis=1,
        )
        select = jnp.where(
            jnp.arange(systems, dtype=jnp.int32)[:, None] == members[None], factors[None], 0.0
        )
        quadrature = jnp.zeros_like(forcing) + jnp.dot(
            select, segment, precision=lax.Precision.HIGHEST
        )
        base = start_value + time_step * quadrature
        defect = base - node_state
        partial_value = jnp.sum(defect * defect, axis=1)
        totals.append(lax.psum(partial_value, ("tm", "node")))
        target = base - implicit * (node_state - node_state * node_state * node_state)
        iterate = node_state
        for newton_step in range(NEWTON):
            cubic = iterate * iterate * iterate
            derivative = 1.0 - implicit + 3.0 * implicit * iterate * iterate
            iterate = iterate - (iterate - implicit * (iterate - cubic) - target) / derivative
        node_state = iterate
    summed = jnp.stack(totals)
    cell_total = lax.axis_size("tm") * M * cells
    residual_log = jnp.log(log_floor + summed / cell_total)
    return (node_state[None, None], residual_log)


def solution(mesh):
    placed = (P("tm", None, None), P())
    return jax.shard_map(
        body,
        mesh=mesh,
        in_specs=placed,
        out_specs=(P("tm", "node", None, None), P()),
        check_vma=False,
    )
```

profile of v0, /device:TPU:0, one launch (start us, length us, event | category | flops | bytes accessed | tf_op | source)
XLA Modules:
  0.0 382.4 jit_solution(9539708886038330631)
XLA Ops:
  7.2 0.0 all-gather.4.cloned.1.call-start
  7.2 0.8 fusion.81
  8.0 0.0 copy-start
  8.0 0.0 copy-start.1
  8.0 3.0 fusion.82
  11.1 0.0 copy-done
  11.1 0.1 slice.52
  11.2 0.4 copy-done.1
  11.5 2.5 fusion
  14.0 0.0 copy-start.5
  14.0 0.0 all-gather.4.cloned.1.call-update
  14.0 0.0 all-reduce.4.cloned.1.call-start
  14.1 6.3 %collective-permute-start = (f32[32,16384]{1,0:T(8,128)}, f32[32,16384]{1,0:T(8,128)}, u32[]{:S(2)}, u32[]{:S(2)}) collective-permute-start(f32[32,16384]{1,0:T(8,128)} %bitcast.26), channel_id=1, source_target_pairs={{0,4},{4,8},{8,12},{12,16},{16,20},{20,24},{24,28},{1,5},{5,9},{9,... | collective-permute-start | bytes 6291464 | tf_op jit(solution)/shard_map/ppermute | solution.py:23
  20.3 0.0 copy-done.5
  20.3 0.6 dynamic_slice.6
  22.2 0.7 dynamic-slice_bitcast_fusion
  22.9 0.1 select_reduce_fusion
  23.0 41.1 %collective-permute-done = f32[32,16384]{1,0:T(8,128)} collective-permute-done((f32[32,16384]{1,0:T(8,128)}, f32[32,16384]{1,0:T(8,128)}, u32[]{:S(2)}, u32[]{:S(2)}) %collective-permute-start) | collective-permute-done | bytes 2097184 | tf_op jit(solution)/shard_map/ppermute | solution.py:23
  64.2 11.0 %all-gather.4.cloned.1.call-done = f32[128,16384]{1,0:T(8,128)} async-done(((f32[32,16384]{1,0:T(8,128)}), f32[128,16384]{1,0:T(8,128)}) %all-gather.4.cloned.1.call-update) | async-done | bytes 8388624 | tf_op jit(solution)/shard_map/all_gather | solution.py:109
  75.2 10.5 %broadcast_select_fusion.1 = (f32[32,16384]{1,0:T(8,128)}, f32[32,16384]{1,0:T(8,128)S(1)}, f32[32]{0:T(128)S(1)}) fusion(pred[]{:T(512)S(6)} %eq.27, f32[]{:T(128)S(6)} %mul.175, f32[]{:T(128)S(6)} %sub.156, f32[32,16384]{1,0:T(8,128)} %collective-permute-done, pred[]{:T(512)S(6)} %eq.20, f32[]{:T(128)} %bitcast.1, f32[1,32,16384]{2,1,0:T(8,128)} %param.4, ...), kind=kOutput, calls=%fused_computation.87 | convolution fusion | flops 821043200 | bytes 16778382 | tf_op jit(solution)/shard_map/dot_general | solution.py:122
  85.6 0.1 fusion.79
  85.7 2.6 fusion.80
  88.3 0.0 copy-done.4
  88.3 0.0 all-reduce.4.cloned.1.call-update
  88.4 0.0 all-gather.6.cloned.1.call-start
  88.4 5.3 %fusion.2 = f32[32,16384]{1,0:T(8,128)} fusion(f32[32,16384]{1,0:T(8,128)} %copy-done.4, f32[32,16384]{1,0:T(8,128)S(1)} %copy-done, f32[32,1]{1,0:T(8,128)S(1)} %get-tuple-element.18, f32[32,16383]{1,0:T(8,128)} %get-tuple-element.20, f32[32,16383]{1,0:T(8,128)} %get-tuple-element.19, f32[32,1]{1,0:T(8,128)S(1)} %get-tuple-element.17, ...), kind=kLoop, calls=%fused_computation.17 | loop fusion | flops 6291456 | bytes 12582912 | tf_op jit(solution)/shard_map/sub | solution.py:82
  93.8 0.0 all-gather.6.cloned.1.call-update
  93.8 0.0 all-reduce.6.cloned.1.call-start
  93.8 46.4 %all-reduce.4.cloned.1.call-done = f32[32,16384]{1,0:T(8,128)} async-done(((f32[32,16384]{1,0:T(8,128)}), f32[32,16384]{1,0:T(8,128)}) %all-reduce.4.cloned.1.call-update) | async-done | bytes 2097168 | tf_op jit(solution)/shard_map/psum | solution.py:17
  140.2 4.7 %collective-permute-start.1 = (f32[32,16384]{1,0:T(8,128)}, f32[32,16384]{1,0:T(8,128)}, u32[]{:S(2)}, u32[]{:S(2)}) collective-permute-start(f32[32,16384]{1,0:T(8,128)} %all-reduce.4.cloned.1.call-done), channel_id=1, source_target_pairs={{0,4},{4,8},{8,12},{12,16},{16,20},{20,24},{24,28},{1,5},{5,9},{9,... | collective-permute-start | bytes 6291464 | tf_op jit(solution)/shard_map/ppermute | solution.py:23
  144.9 43.6 %collective-permute-done.1 = f32[32,16384]{1,0:T(8,128)} collective-permute-done((f32[32,16384]{1,0:T(8,128)}, f32[32,16384]{1,0:T(8,128)}, u32[]{:S(2)}, u32[]{:S(2)}) %collective-permute-start.1) | collective-permute-done | bytes 2097184 | tf_op jit(solution)/shard_map/ppermute | solution.py:23
  188.5 11.6 %all-gather.6.cloned.1.call-done = f32[128,16384]{1,0:T(8,128)} async-done(((f32[32,16384]{1,0:T(8,128)}), f32[128,16384]{1,0:T(8,128)}) %all-gather.6.cloned.1.call-update) | async-done | bytes 8388624 | tf_op jit(solution)/shard_map/all_gather | solution.py:109
  200.1 10.8 %broadcast_select_fusion = (f32[32,16384]{1,0:T(8,128)}, f32[32,16384]{1,0:T(8,128)S(1)}, f32[32]{0:T(128)S(1)}) fusion(pred[]{:T(512)S(6)} %eq.27, f32[32,16384]{1,0:T(8,128)} %copy-done.4, f32[]{:T(128)S(6)} %mul.175, f32[]{:T(128)S(6)} %sub.156, f32[]{:T(128)} %bitcast.1, f32[128,16384]{1,0:T(8,128)} %all-gather.6.cloned.1.call-done, ...), kind=kOutput, calls=%fused_computation.86 | convolution fusion | flops 821043200 | bytes 18875534 | tf_op jit(solution)/shard_map/dot_general | solution.py:122
  210.9 0.1 fusion.77
  211.0 2.6 fusion.78
  213.6 0.0 copy-done.3
  213.6 0.0 all-reduce.6.cloned.1.call-update
  213.7 0.2 all-gather.8.cloned.1.call-start
  213.9 5.3 %fusion.4 = f32[32,16384]{1,0:T(8,128)} fusion(f32[32,16384]{1,0:T(8,128)} %copy-done.3, f32[32,16384]{1,0:T(8,128)S(1)} %copy-done, f32[32,1]{1,0:T(8,128)S(1)} %get-tuple-element.14, f32[32,16383]{1,0:T(8,128)} %get-tuple-element.16, f32[32,16383]{1,0:T(8,128)} %get-tuple-element.15, f32[32,1]{1,0:T(8,128)S(1)} %get-tuple-element.13, ...), kind=kLoop, calls=%fused_computation.19 | loop fusion | flops 6291456 | bytes 12582912 | tf_op jit(solution)/shard_map/sub | solution.py:82
  219.2 0.0 all-gather.8.cloned.1.call-update
  219.3 46.2 %all-reduce.6.cloned.1.call-done = f32[32,16384]{1,0:T(8,128)} async-done(((f32[32,16384]{1,0:T(8,128)}), f32[32,16384]{1,0:T(8,128)}) %all-reduce.6.cloned.1.call-update) | async-done | bytes 2097168 | tf_op jit(solution)/shard_map/psum | solution.py:17
  265.5 4.7 %collective-permute-start.2 = (f32[32,16384]{1,0:T(8,128)}, f32[32,16384]{1,0:T(8,128)}, u32[]{:S(2)}, u32[]{:S(2)}) collective-permute-start(f32[32,16384]{1,0:T(8,128)} %all-reduce.6.cloned.1.call-done), channel_id=1, source_target_pairs={{0,4},{4,8},{8,12},{12,16},{16,20},{20,24},{24,28},{1,5},{5,9},{9,... | collective-permute-start | bytes 6291464 | tf_op jit(solution)/shard_map/ppermute | solution.py:23
  270.2 43.6 %collective-permute-done.2 = f32[32,16384]{1,0:T(8,128)} collective-permute-done((f32[32,16384]{1,0:T(8,128)}, f32[32,16384]{1,0:T(8,128)}, u32[]{:S(2)}, u32[]{:S(2)}) %collective-permute-start.2) | collective-permute-done | bytes 2097184 | tf_op jit(solution)/shard_map/ppermute | solution.py:23
  313.8 11.5 %all-gather.8.cloned.1.call-done = f32[128,16384]{1,0:T(8,128)} async-done(((f32[32,16384]{1,0:T(8,128)}), f32[128,16384]{1,0:T(8,128)}) %all-gather.8.cloned.1.call-update) | async-done | bytes 8388624 | tf_op jit(solution)/shard_map/all_gather | solution.py:109
  325.3 0.0 copy-done.2
  325.3 10.4 %multiply_reduce_fusion = (f32[32]{0:T(128)S(1)}, f32[1,1,32,16384]{3,2,1,0:T(8,128)}) fusion(f32[32,16384]{1,0:T(8,128)} %copy-done.3, f32[]{:T(128)S(6)} %mul.175, f32[]{:T(128)S(6)} %sub.156, f32[]{:T(128)} %bitcast.1, f32[128,16384]{1,0:T(8,128)} %all-gather.8.cloned.1.call-done, f32[128]{0:T(128)S(1)} %select_reduce_fusion, ...), kind=kOutput, calls=%fused_computation.79 | convolution fusion | flops 820518912 | bytes 16778380 | tf_op jit(solution)/shard_map/dot_general | solution.py:122
  335.7 39.6 %all-reduce = (f32[1,32]{1,0:T(1,128)S(1)}, f32[1,32]{1,0:T(1,128)S(1)}, f32[1,32]{1,0:T(1,128)S(1)}) all-reduce(f32[1,32]{1,0:T(1,128)S(1)} %bitcast.29, f32[1,32]{1,0:T(1,128)S(1)} %bitcast.28, f32[1,32]{1,0:T(1,128)S(1)} %bitcast.27), channel_id=1, replica_groups=mesh['tm'=8,'node'=4] {'tm','node'}, use_global_device_ids=true, to_apply=%region_8.9 | all-reduce | flops 96 | bytes 768 | tf_op jit(solution)/shard_map/psum | solution.py:128
  375.3 0.6 fusion.71
  (5 shorter events, 0.0 us)
Async XLA Ops:
  7.2 68.0 %all-gather.4.cloned.1.call-start = ((), (), s32[]{:S(2)}) async-start(), calls=%async_computation | async-start | bytes 10485760 | tf_op jit(solution)/shard_map/all_gather | solution.py:109
  8.0 3.1 copy-start
  8.0 3.5 copy-start.1
  14.0 6.4 %copy-start.5 = (f32[4]{0:T(128)S(1)}, f32[4]{0:T(128)}, u32[]{:S(2)}) copy-start(f32[4]{0:T(128)} %constant.74.clone) | copy-start | bytes 52
  14.0 126.2 %all-reduce.4.cloned.1.call-start = ((), (), s32[]{:S(2)}) async-start(), calls=%async_computation.1 | async-start | bytes 4194304 | tf_op jit(solution)/shard_map/psum | solution.py:17
  14.1 50.1 %collective-permute-start = (f32[32,16384]{1,0:T(8,128)}, f32[32,16384]{1,0:T(8,128)}, u32[]{:S(2)}, u32[]{:S(2)}) collective-permute-start(f32[32,16384]{1,0:T(8,128)} %bitcast.26), channel_id=1, source_target_pairs={{0,4},{4,8},{8,12},{12,16},{16,20},{20,24},{24,28},{1,5},{5,9},{9,... | collective-permute-start | bytes 6291464 | tf_op jit(solution)/shard_map/ppermute | solution.py:23
  85.6 2.7 copy-start.4
  88.4 111.8 %all-gather.6.cloned.1.call-start = ((), (), s32[]{:S(2)}) async-start(), calls=%async_computation.2 | async-start | bytes 10485760 | tf_op jit(solution)/shard_map/all_gather | solution.py:109
  93.8 171.7 %all-reduce.6.cloned.1.call-start = ((), (), s32[]{:S(2)}) async-start(), calls=%async_computation.3 | async-start | bytes 4194304 | tf_op jit(solution)/shard_map/psum | solution.py:17
  140.2 48.3 %collective-permute-start.1 = (f32[32,16384]{1,0:T(8,128)}, f32[32,16384]{1,0:T(8,128)}, u32[]{:S(2)}, u32[]{:S(2)}) collective-permute-start(f32[32,16384]{1,0:T(8,128)} %all-reduce.4.cloned.1.call-done), channel_id=1, source_target_pairs={{0,4},{4,8},{8,12},{12,16},{16,20},{20,24},{24,28},{1,5},{5,9},{9,... | collective-permute-start | bytes 6291464 | tf_op jit(solution)/shard_map/ppermute | solution.py:23
  210.9 2.7 copy-start.3
  213.7 111.6 %all-gather.8.cloned.1.call-start = ((), (), s32[]{:S(2)}) async-start(), calls=%async_computation.4 | async-start | bytes 10485760 | tf_op jit(solution)/shard_map/all_gather | solution.py:109
  219.2 106.0 %copy-start.2 = (f32[1,32,16384]{2,1,0:T(8,128)S(1)}, f32[1,32,16384]{2,1,0:T(8,128)}, u32[]{:S(2)}) copy-start(f32[1,32,16384]{2,1,0:T(8,128)} %param.4) | copy-start | bytes 6291460
  265.5 48.3 %collective-permute-start.2 = (f32[32,16384]{1,0:T(8,128)}, f32[32,16384]{1,0:T(8,128)}, u32[]{:S(2)}, u32[]{:S(2)}) collective-permute-start(f32[32,16384]{1,0:T(8,128)} %all-reduce.6.cloned.1.call-done), channel_id=1, source_target_pairs={{0,4},{4,8},{8,12},{12,16},{16,20},{20,24},{24,28},{1,5},{5,9},{9,... | collective-permute-start | bytes 6291464 | tf_op jit(solution)/shard_map/ppermute | solution.py:23
Sparse Core Ops, SparseCore 0:
  14.1 60.9 all-gather.3
  88.5 51.6 all-reduce.3
  141.8 58.3 all-gather.5
  213.8 51.6 all-reduce.5
  266.9 58.3 all-gather.7
where the time goes:
time: 383 us; the launch traced here: 382 us
  waiting for transfers between devices  255 us (67%)
  blocking collectives  39.6 us (10%)
  matrix products  31.7 us (8%)
  starting transfers between devices  16 us (4%)
  between operations  15.1 us (4%)
  other arithmetic  13.9 us (4%)
  local copies, waits for them, and re-layouts  10.9 us (3%)
    ppermute x3, waiting for transfers between devices, passed_along(): return lax.ppermute(value, axis, pairs)  128 us
    psum x2, waiting for transfers between devices, spread(): return lax.psum(jnp.where(mine, value, jnp.zeros_like(value)), axis)  92.6 us
    psum x1, blocking collectives, body(): totals.append(lax.psum(partial_value, ('tm', 'node')))  39.6 us
    all_gather x3, waiting for transfers between devices, body(): segment = lax.all_gather(forcing, 'node', axis=0, tiled=True)  34.1 us
    dot_general x3, matrix products, body(): jnp.dot(select, segment, precision=lax.Precision.HIGHEST)  31.7 us
    ppermute x3, starting transfers between devices, passed_along(): return lax.ppermute(value, axis, pairs)  15.6 us
    sub x3, other arithmetic, operator_term(): coupling * (right_side - field_values)  13.2 us
    slice x6, local copies, waits for them, and re-layouts, operator_term(): left_side = jnp.roll(field_values, 1, axis=-1)  9.22 us
  transfers between devices with their start and end apart: 8, of which 8 were waited for; matrix products, arithmetic and copies ran while one was open for 3% of the time, Pallas kernels for 0%

commit v1 on v0

v1 whole, which is shorter than its diff:
```python
import functools

import jax
import jax.numpy as jnp
from jax import lax
from jax.experimental import pallas as pl
from jax.experimental.pallas import tpu as pltpu
from jax.sharding import PartitionSpec as P


M = 4
SWEEPS = 3
NEWTON = 2
LANES = 128
CHUNKS = 2
GROUP = 17
LARGE_LIMIT = 24 * 1024 * 1024
SMALL_LIMIT = 8 * 1024 * 1024

time_step = 0.5
log_floor = 0.05


def legendre_gap(point, node_count):
    before = 1.0
    current = point
    for degree in range(1, node_count):
        following = ((2 * degree + 1) * point * current - degree * before) / (degree + 1)
        before = current
        current = following
    return current - before


def collocation(node_count):
    points = []
    samples = 4000
    for sample_index in range(samples - 1):
        lower_end = -1.0 + 2.0 * sample_index / samples
        upper_end = -1.0 + 2.0 * (sample_index + 1) / samples
        lower_value = legendre_gap(lower_end, node_count)
        upper_value = legendre_gap(upper_end, node_count)
        if lower_value * upper_value < 0.0:
            for _ in range(80):
                middle = 0.5 * (lower_end + upper_end)
                middle_value = legendre_gap(middle, node_count)
                if lower_value * middle_value <= 0.0:
                    upper_end = middle
                else:
                    lower_end = middle
                    lower_value = middle_value
            points.append(0.5 * (lower_end + upper_end))
    points.append(1.0)
    node_times = [(point + 1.0) / 2.0 for point in points]
    matrix = [[0.0] * node_count for _ in range(node_count)]
    for column in range(node_count):
        coeffs = [1.0]
        for other in range(node_count):
            if other != column:
                scale = node_times[column] - node_times[other]
                shifted = [0.0] + coeffs
                scaled = [value * node_times[other] for value in coeffs] + [0.0]
                coeffs = [(shifted[power] - scaled[power]) / scale for power in range(len(shifted))]
        for row_index in range(node_count):
            upper_time = node_times[row_index]
            matrix[row_index][column] = sum(
                (
                    coeffs[power] * upper_time ** (power + 1) / (power + 1)
                    for power in range(len(coeffs))
                )
            )
    return (node_times, matrix)


NODE_TIMES, MATRIX = collocation(M)
LAST = M - 1
WEIGHTS = [[time_step * entry for entry in row] for row in MATRIX]
ROW_SUMS = [time_step * moment for moment in NODE_TIMES]
IMPLICIT = [time_step * moment / M for moment in NODE_TIMES]


def newton_steps(base, value, square, weight):
    rest = base - weight * value
    tripled = square * (3.0 * weight)
    cubic = tripled * value
    target = rest + cubic * (1.0 / 3.0)
    value = (rest + cubic) / (tripled + (1.0 - weight))
    for _ in range(1, NEWTON):
        tripled = (value * value) * (3.0 * weight)
        numerator = target + (tripled * value) * (2.0 / 3.0)
        value = numerator / (tripled + (1.0 - weight))
    return value


def weighted(terms, row):
    total = terms[0] * row[0]
    for term, entry in zip(terms[1:], row[1:]):
        total = total + term * entry
    return total


def group_of(count):
    return max(size for size in range(1, GROUP + 1) if count % size == 0)


def lanes_at(offset):
    return pl.ds(pl.multiple_of(offset, LANES), LANES)


def tracks(source, target, row, column, cells, core, sem):
    rows = target.shape[0]
    part = source.at[pl.ds(pl.multiple_of(row, rows), rows), :]
    before = pl.multiple_of(lax.rem(column + (cells - LANES), cells), LANES)
    after = pl.multiple_of(lax.rem(column + core, cells), LANES)
    middle = pl.multiple_of(column, LANES)
    return [
        pltpu.make_async_copy(
            part.at[:, pl.ds(before, LANES)], target.at[:, pl.ds(0, LANES)], sem.at[0]
        ),
        pltpu.make_async_copy(
            part.at[:, pl.ds(middle, core)], target.at[:, pl.ds(LANES, core)], sem.at[1]
        ),
        pltpu.make_async_copy(
            part.at[:, pl.ds(after, LANES)],
            target.at[:, pl.ds(LANES + core, LANES)],
            sem.at[2],
        ),
    ]


def place():
    position = lax.axis_index("tm")
    return lax.rem(position, 2), lax.div(position, 2), lax.axis_index("node")


def split_kernel(starts, couplings, mine, other, near, sems):
    side, _, node = place()
    rows, length = mine.shape
    cells = starts.shape[1]
    core = length - 2 * LANES
    copies = []
    for slot, (source, target, which) in enumerate(
        ((starts, mine, side), (starts, other, 1 - side), (couplings, near, side))
    ):
        copies += tracks(source, target, node * rows, which * core, cells, core, sems.at[slot])
    for copy in copies:
        copy.start()
    for copy in copies:
        copy.wait()


def split_starts(starts, couplings, rows, length):
    return pl.pallas_call(
        split_kernel,
        out_shape=[jax.ShapeDtypeStruct((rows, length), jnp.float32)] * 3,
        in_specs=[pl.BlockSpec(memory_space=pltpu.HBM)] * 2,
        out_specs=[pl.BlockSpec(memory_space=pltpu.VMEM)] * 3,
        scratch_shapes=[pltpu.SemaphoreType.DMA((3, 3))],
        compiler_params=pltpu.CompilerParams(vmem_limit_bytes=SMALL_LIMIT),
        cost_estimate=pl.CostEstimate(
            flops=rows * length, bytes_accessed=24 * rows * length, transcendentals=0
        ),
        name="split",
    )(starts, couplings)


def edge_masks(rows):
    lane = lax.broadcasted_iota(jnp.int32, (rows, LANES), 1)
    return lane, lane == 0, lane == LANES - 1


def over(rows, length, base, visits):
    count = length // LANES - 2 * base
    size = group_of(count)

    def step(group, totals):
        start = (base + group * size) * LANES
        totals = list(totals)

        def tile_at(tile):
            offset = start + tile * LANES
            if base == 0 and tile < 0:
                offset = jnp.maximum(offset, 0)
            if base == 0 and tile >= size:
                offset = jnp.minimum(offset, length - LANES)
            return lanes_at(offset)

        for tile in range(size):
            for index, visit in enumerate(visits):
                share = visit(tile_at, tile)
                if share is None:
                    continue
                if base == 0 and tile == 0:
                    share = jnp.where(group == 0, 0.0, share)
                if base == 0 and tile == size - 1:
                    share = jnp.where(group == count // size - 1, 0.0, share)
                totals[index] = totals[index] + share
        return tuple(totals)

    zero = jnp.zeros((rows, LANES), jnp.float32)
    return lax.fori_loop(0, count // size, step, (zero,) * len(visits))


def keep(ref):
    def store(index, at, value):
        ref[0, index, :, at] = value
        ref[1, index, :, at] = pltpu.roll(value, LANES - 1, 1)
        ref[2, index, :, at] = pltpu.roll(value, 1, 1)

    return store


def opening(coupling, left_coupling, start, refs, store, nodes):
    _, is_first, is_last = edge_masks(coupling.shape[0])
    here, ahead, behind = refs

    def visit(tile_at, tile):
        at, above, below = tile_at(tile), tile_at(tile + 1), tile_at(tile - 1)
        value = here[:, at]
        right = jnp.where(is_last, ahead[:, above], ahead[:, at])
        left = jnp.where(is_first, behind[:, below], behind[:, at])
        square = value * value
        flow = coupling[:, at] * (right - value) - left_coupling[:, at] * (value - left)
        slope = flow + (value - value * square)
        origin = start(at)
        share = None
        for index in nodes:
            base = origin + slope * ROW_SUMS[index]
            defect = base - value
            share = defect * defect if share is None else share + defect * defect
            store(index, at, newton_steps(base, value, square, IMPLICIT[index]))
        return share

    return visit


def later(coupling, left_coupling, start, ref, store, nodes):
    _, is_first, is_last = edge_masks(coupling.shape[0])

    def visit(tile_at, tile):
        at, above, below = tile_at(tile), tile_at(tile + 1), tile_at(tile - 1)
        values, squares, slopes = [], [], []
        for index in range(M):
            value = ref[0, index, :, at]
            right = jnp.where(is_last, ref[1, index, :, above], ref[1, index, :, at])
            left = jnp.where(is_first, ref[2, index, :, below], ref[2, index, :, at])
            square = value * value
            flow = coupling[:, at] * (right - value) - left_coupling[:, at] * (value - left)
            values.append(value)
            squares.append(square)
            slopes.append(flow + (value - value * square))
        origin = start(at)
        share = None
        for index in nodes:
            base = origin + weighted(slopes, WEIGHTS[index])
            defect = base - values[index]
            share = defect * defect if share is None else share + defect * defect
            store(index, at, newton_steps(base, values[index], squares[index], IMPLICIT[index]))
        return share

    return visit


def inner(at):
    return pl.ds(at.start - LANES, LANES)


def emit(done):
    def store(index, at, value):
        done[index, :, inner(at)] = value

    return store


def shifted_by(at, offset):
    return lanes_at(at.start + offset)


def early_kernel(
    chunk, near, mine, partner, straight, crossed,
    ending, w_lo, coupling, left_coupling, done, residual,
    v_lo, v_lo_ahead, v_lo_behind, v_hi, v_hi_ahead, v_hi_behind,
    v_h1, v_h1_ahead, v_h1_behind, v_h2, e_h1, u_lo, u_hi, w_hi,
):
    side, pair, _ = place()
    first = pair == 0
    even = side == 0
    rows, length = coupling.shape
    core = length - 2 * LANES
    _, is_first, _ = edge_masks(rows)

    def prepare(tile_at, tile):
        at, below = tile_at(tile), tile_at(tile - 1)
        wide = shifted_by(at, chunk * core)
        own = near[:, wide]
        coupling[:, at] = own
        left_coupling[:, at] = jnp.where(
            is_first, pltpu.roll(near[:, shifted_by(below, chunk * core)], 1, 1),
            pltpu.roll(own, 1, 1),
        )
        for pick, here, ahead, behind in (
            ((mine, partner), v_lo, v_lo_ahead, v_lo_behind),
            ((partner, mine), v_hi, v_hi_ahead, v_hi_behind),
            ((crossed, straight), v_h1, v_h1_ahead, v_h1_behind),
        ):
            value = jnp.where(even, pick[0][:, wide], pick[1][:, wide])
            here[:, at] = value
            ahead[:, at] = pltpu.roll(value, LANES - 1, 1)
            behind[:, at] = pltpu.roll(value, 1, 1)
        v_h2[:, at] = jnp.where(even, straight[:, wide], crossed[:, wide])

    over(rows, length, 0, [prepare])

    def keep_end(index, at, value):
        e_h1[:, at] = value

    pieces = (coupling, left_coupling)
    every = range(M)
    _, lo_0, hi_0 = over(
        rows,
        length,
        0,
        [
            opening(
                *pieces, lambda s: v_h2[:, s], (v_h1, v_h1_ahead, v_h1_behind), keep_end, [LAST]
            ),
            opening(
                *pieces,
                lambda s: jnp.where(first, v_lo[:, s], v_h1[:, s]),
                (v_lo, v_lo_ahead, v_lo_behind), keep(u_lo), every,
            ),
            opening(
                *pieces, lambda s: v_lo[:, s], (v_hi, v_hi_ahead, v_hi_behind), keep(u_hi), every
            ),
        ],
    )
    lo_1, hi_1 = over(
        rows,
        length,
        0,
        [
            later(
                *pieces,
                lambda s: jnp.where(first, v_lo[:, s], e_h1[:, s]),
                u_lo, keep(w_lo), every,
            ),
            later(*pieces, lambda s: u_lo[0, LAST, :, s], u_hi, keep(w_hi), every),
        ],
    )

    def last(tile_at, tile):
        at = tile_at(tile)
        ending[:, inner(at)] = w_hi[0, LAST, :, at]
        return third(tile_at, tile)

    third = later(*pieces, lambda s: w_lo[0, LAST, :, s], w_hi, emit(done), every)
    (hi_2,) = over(rows, length, 1, [last])
    residual[0] = lo_0 + hi_0
    residual[1] = lo_1 + hi_1
    residual[2] = hi_2


def late_kernel(
    chunk, mine, partner, ending, w_lo, coupling, left_coupling, done, before, *refs
):
    outs, (residual, fresh) = refs[: 2 * M], refs[2 * M :]
    side, pair, node = place()
    first = pair == 0
    even = side == 0
    rows, length = coupling.shape
    core = length - 2 * LANES

    def start(s):
        wide = shifted_by(s, chunk * core)
        begun = jnp.where(even, mine[:, wide], partner[:, wide])
        return jnp.where(first, begun, ending[:, inner(s)])

    (lo_2,) = over(
        rows,
        length,
        1,
        [later(coupling, left_coupling, start, w_lo, emit(fresh), range(M))],
    )
    residual[0] = before[0]
    residual[1] = before[1]
    residual[2] = before[2] + lo_2

    def hand_over(lo_flip):
        def copy(tile_at, tile):
            at = inner(tile_at(tile))
            for other in range(M):
                outs[lo_flip * M + other][:, at] = fresh[other ^ node, :, at]
                outs[(1 - lo_flip) * M + other][:, at] = done[other ^ node, :, at]

        over(rows, length, 1, [copy])

    for index in range(2):

        @pl.when(side == index)
        def _(index=index):
            hand_over(index)


def run_early(chunk, near, pieces, core):
    rows = near.shape[0]
    length = core + 2 * LANES
    shape = jax.ShapeDtypeStruct
    flat = pltpu.VMEM((rows, length), jnp.float32)
    deep = pltpu.VMEM((3, M, rows, length), jnp.float32)
    vmem = pl.BlockSpec(memory_space=pltpu.VMEM)
    return pl.pallas_call(
        functools.partial(early_kernel, chunk),
        out_shape=[
            shape((rows, core), jnp.float32),
            shape((3, M, rows, length), jnp.float32),
            shape((rows, length), jnp.float32),
            shape((rows, length), jnp.float32),
            shape((M, rows, core), jnp.float32),
            shape((SWEEPS, rows, LANES), jnp.float32),
        ],
        in_specs=[vmem] * (1 + len(pieces)),
        out_specs=[vmem] * 6,
        scratch_shapes=[flat] * 11 + [deep] * 3,
        compiler_params=pltpu.CompilerParams(vmem_limit_bytes=LARGE_LIMIT),
        cost_estimate=pl.CostEstimate(
            flops=800 * rows * length, bytes_accessed=64 * rows * length, transcendentals=0
        ),
        name="early",
    )(near, *pieces)


def run_late(chunk, mine, partner, ending, state):
    rows, core = ending.shape
    shape = jax.ShapeDtypeStruct
    vmem = pl.BlockSpec(memory_space=pltpu.VMEM)
    results = pl.pallas_call(
        functools.partial(late_kernel, chunk),
        out_shape=[shape((rows, core), jnp.float32)] * (2 * M)
        + [shape((SWEEPS, rows, LANES), jnp.float32)],
        in_specs=[vmem] * (3 + len(state)),
        out_specs=[vmem] * (2 * M + 1),
        scratch_shapes=[pltpu.VMEM((M, rows, core), jnp.float32)],
        compiler_params=pltpu.CompilerParams(vmem_limit_bytes=LARGE_LIMIT),
        cost_estimate=pl.CostEstimate(
            flops=200 * rows * core, bytes_accessed=64 * rows * core, transcendentals=0
        ),
        name="late",
    )(mine, partner, ending, *state)
    return results[: 2 * M], results[2 * M]


def gather_kernel(half, start, count, *refs):
    blocks = refs[:count]
    out, save = refs[-2:]
    side, _, node = place()
    rows, chunk = blocks[0].shape
    copies = []
    for index, block in enumerate(blocks):
        flip, other = index // M, index % M
        column = (side if flip == 0 else 1 - side) * half + start
        target = out.at[
            pl.ds(pl.multiple_of((other ^ node) * rows, rows), rows),
            pl.ds(pl.multiple_of(column, LANES), chunk),
        ]
        copies.append(pltpu.make_async_copy(block, target, save.at[index]))
    for copy in copies:
        copy.start()
    for copy in copies:
        copy.wait()


def gather_blocks(blocks, result, half, start, systems):
    rows, chunk = blocks[0].shape
    count = len(blocks)
    hbm = pl.BlockSpec(memory_space=pltpu.HBM)
    vmem = pl.BlockSpec(memory_space=pltpu.VMEM)
    previous = [] if result is None else [result]
    return pl.pallas_call(
        functools.partial(gather_kernel, half, start, count),
        out_shape=jax.ShapeDtypeStruct((systems, 2 * half), jnp.float32),
        in_specs=[vmem] * count + [hbm] * len(previous),
        out_specs=hbm,
        scratch_shapes=[pltpu.SemaphoreType.DMA((count,))],
        input_output_aliases={} if result is None else {count: 0},
        compiler_params=pltpu.CompilerParams(vmem_limit_bytes=SMALL_LIMIT),
        cost_estimate=pl.CostEstimate(
            flops=count * rows * chunk, bytes_accessed=8 * count * rows * chunk, transcendentals=0
        ),
        name="assemble",
    )(*blocks, *previous)


def body(slice_starts, coupling):
    slices = lax.axis_size("tm")
    systems, cells = coupling.shape
    rows = systems // M
    half = cells // 2
    chunk = half // CHUNKS
    count = slices * M

    def moved(value, target):
        pairs = [(i, target(i)) for i in range(slices)]
        return lax.ppermute(value, "tm", [(i, j) for i, j in pairs if 0 <= j < slices])

    mine, other, near = split_starts(slice_starts[0], coupling, rows, half + 2 * LANES)
    pieces = (
        mine,
        moved(other, lambda i: i ^ 1),
        moved(mine, lambda i: i + 2),
        moved(other, lambda i: (i ^ 1) + 2),
    )
    states, endings = [], []
    for index in range(CHUNKS):
        ending, *state = run_early(index, near, pieces, chunk)
        endings.append(moved(ending, lambda i: i + 2))
        states.append(state)
    partial = None
    result = None
    for index in range(CHUNKS):
        outs, sums = run_late(index, pieces[0], pieces[1], endings[index], states[index])
        partial = sums if partial is None else partial + sums
        blocks = [outs[0]]
        for step in range(1, 2 * M):
            pairs = [(i, i ^ step) for i in range(count)]
            blocks.append(lax.ppermute(outs[step], ("tm", "node"), pairs))
        result = gather_blocks(blocks, result, half, index * chunk, systems)

    sums = jnp.sum(partial, axis=2)
    flat = jnp.pad(sums.reshape(-1), (0, -sums.size % LANES))
    shared = lax.all_to_all(
        jnp.broadcast_to(flat[None], (count, flat.shape[0])), ("tm", "node"), 0, 0
    )
    summed = jnp.sum(shared.reshape(slices, M, -1), axis=0)[:, : sums.size]
    summed = summed.reshape(M, SWEEPS, rows).transpose(1, 0, 2).reshape(SWEEPS, systems)
    residual_log = jnp.log(log_floor + summed / (slices * M * cells))
    return (result[None, None], residual_log)


def solution(mesh):
    placed = (P("tm", None, None), P())

    return jax.shard_map(
        body,
        mesh=mesh,
        in_specs=placed,
        out_specs=(P("tm", "node", None, None), P()),
        check_vma=False,
    )
```

time: 383 us -> 73.9 us (0.19)
  waiting for transfers between devices: 255 us -> 14 us
  matrix products: 31.7 us -> 0 us
  blocking collectives: 39.6 us -> 8.87 us
  starting transfers between devices: 16 us -> 33.5 us
  between operations: 15.1 us -> 0.76 us
  other arithmetic: 13.9 us -> 0.11 us
  Pallas kernels: 0 us -> 12.3 us
  local copies, waits for them, and re-layouts: 10.9 us -> 4.04 us
    ppermute x3 -> x19, waiting for transfers between devices: 128 us -> 14 us  [the longest x14 7.49 us: body(): blocks.append(lax.ppermute(outs[step], ('tm', 'node'), pairs))]
    psum x2 -> x0, waiting for transfers between devices: 92.6 us -> none  [spread(): return lax.psum(jnp.where(mine, value, jnp.zeros_like(value)), axis)]
    psum x1 -> x0, blocking collectives: 39.6 us -> none  [body(): totals.append(lax.psum(partial_value, ('tm', 'node')))]
    all_gather x3 -> x0, waiting for transfers between devices: 34.1 us -> none  [body(): segment = lax.all_gather(forcing, 'node', axis=0, tiled=True)]
    dot_general x3 -> x0, matrix products: 31.7 us -> none  [body(): jnp.dot(select, segment, precision=lax.Precision.HIGHEST)]
    ppermute x3 -> x19, starting transfers between devices: 15.6 us -> 33.5 us  [the longest x5 19.2 us: moved(): lax.ppermute(value, 'tm', [(i, j) for i, j in pairs if 0 <= j < slices])]
    sub x3 -> x0, other arithmetic: 13.2 us -> none  [operator_term(): coupling * (right_side - field_values)]
    pallas_call x0 -> x7, Pallas kernels: none -> 12.3 us  [the longest x2 8.04 us: run_early(): pl.pallas_call(functools.partial(early_kernel, chunk), out_shape=[shape((...]
  transfers between devices with their start and end apart: 8 -> 19, of which waited for: 8 -> 8; matrix products, arithmetic and copies ran while one was open for 3% -> 1% of each run, Pallas kernels for 0% -> 10%
where the time goes in v1:
time: 73.9 us; the launch traced here: 73.7 us
  starting transfers between devices  33.5 us (45%)
  waiting for transfers between devices  14 us (19%)
  Pallas kernels  12.3 us (17%)
  blocking collectives  8.87 us (12%)
  local copies, waits for them, and re-layouts  4.04 us (5%)
  between operations  0.76 us (1%)
    ppermute x5, starting transfers between devices, moved(): lax.ppermute(value, 'tm', [(i, j) for i, j in pairs if 0 <= j < slices])  19.2 us
    ppermute x14, starting transfers between devices, body(): blocks.append(lax.ppermute(outs[step], ('tm', 'node'), pairs))  14.3 us
    all_to_all x1, blocking collectives, body(): lax.all_to_all(jnp.broadcast_to(flat[None], (count, flat.shape[0])), ('tm...  8.87 us
    pallas_call x2, Pallas kernels, run_early(): pl.pallas_call(functools.partial(early_kernel, chunk), out_shape=[shape((...  8.04 us
    ppermute x14, waiting for transfers between devices, body(): blocks.append(lax.ppermute(outs[step], ('tm', 'node'), pairs))  7.49 us
    ppermute x5, waiting for transfers between devices, moved(): lax.ppermute(value, 'tm', [(i, j) for i, j in pairs if 0 <= j < slices])  6.54 us
    unnamed x4, local copies, waits for them, and re-layouts  3.17 us
    pallas_call x2, Pallas kernels, gather_blocks(): pl.pallas_call(functools.partial(gather_kernel, half, start, count), out_...  2.05 us
  transfers between devices with their start and end apart: 19, of which 8 were waited for; matrix products, arithmetic and copies ran while one was open for 1% of the time, Pallas kernels for 10%

profile of v1, /device:TPU:0, one launch (start us, length us, event | category | flops | bytes accessed | tf_op | source)
XLA Modules:
  0.0 73.7 jit_solution(6326742138795890628)
XLA Ops:
  0.6 1.6 %copy-done = f32[1,32,16384]{2,1,0:T(8,128)S(1)} copy-done((f32[1,32,16384]{2,1,0:T(8,128)S(1)}, f32[1,32,16384]{2,1,0:T(8,128)}, u32[]{:S(2)}) %copy-start) | copy-done | bytes 2097176
  2.2 1.6 %copy-done.1 = f32[32,16384]{1,0:T(8,128)S(1)} copy-done((f32[32,16384]{1,0:T(8,128)S(1)}, f32[32,16384]{1,0:T(8,128)}, u32[]{:S(2)}) %copy-start.1) | copy-done | bytes 2097176
  3.8 0.2 split.1
  4.0 5.0 %collective-permute-start.1 = (f32[8,8448]{1,0:T(8,128)S(1)}, f32[8,8448]{1,0:T(8,128)S(1)}, u32[]{:S(2)}, u32[]{:S(2)}) collective-permute-start(f32[8,8448]{1,0:T(8,128)S(1)} %get-tuple-element.35.mine), channel_id=1, source_target_pairs={{0,8},{4,12},{8,16},{12,20},{16,24},{20,28},{1,9},{5,13},{9,17},{1... | collective-permute-start | bytes 811016 | tf_op jit(solution)/shard_map/ppermute | solution.py:502
  9.0 1.6 %collective-permute-start = (f32[8,8448]{1,0:T(8,128)S(1)}, f32[8,8448]{1,0:T(8,128)S(1)}, u32[]{:S(2)}, u32[]{:S(2)}) collective-permute-start(f32[8,8448]{1,0:T(8,128)S(1)} %get-tuple-element.36), channel_id=1, source_target_pairs={{0,4},{4,0},{8,12},{12,8},{16,20},{20,16},{24,28},{28,24},{1,5},{5... | collective-permute-start | bytes 811016 | tf_op jit(solution)/shard_map/ppermute | solution.py:502
  10.6 3.4 %collective-permute-start.2 = (f32[8,8448]{1,0:T(8,128)S(1)}, f32[8,8448]{1,0:T(8,128)S(1)}, u32[]{:S(2)}, u32[]{:S(2)}) collective-permute-start(f32[8,8448]{1,0:T(8,128)S(1)} %get-tuple-element.36), channel_id=1, source_target_pairs={{0,12},{4,8},{8,20},{12,16},{16,28},{20,24},{1,13},{5,9},{9,21},{1... | collective-permute-start | bytes 811016 | tf_op jit(solution)/shard_map/ppermute | solution.py:502
  14.0 1.8 %collective-permute-done.1.straight = f32[8,8448]{1,0:T(8,128)S(1)} collective-permute-done((f32[8,8448]{1,0:T(8,128)S(1)}, f32[8,8448]{1,0:T(8,128)S(1)}, u32[]{:S(2)}, u32[]{:S(2)}) %collective-permute-start.1) | collective-permute-done | bytes 270368 | tf_op jit(solution)/shard_map/ppermute | solution.py:502
  15.8 1.2 %collective-permute-done.partner = f32[8,8448]{1,0:T(8,128)S(1)} collective-permute-done((f32[8,8448]{1,0:T(8,128)S(1)}, f32[8,8448]{1,0:T(8,128)S(1)}, u32[]{:S(2)}, u32[]{:S(2)}) %collective-permute-start) | collective-permute-done | bytes 270368 | tf_op jit(solution)/shard_map/ppermute | solution.py:502
  17.0 3.5 %collective-permute-done.2.crossed = f32[8,8448]{1,0:T(8,128)S(1)} collective-permute-done((f32[8,8448]{1,0:T(8,128)S(1)}, f32[8,8448]{1,0:T(8,128)S(1)}, u32[]{:S(2)}, u32[]{:S(2)}) %collective-permute-start.2) | collective-permute-done | bytes 270368 | tf_op jit(solution)/shard_map/ppermute | solution.py:502
  20.5 4.0 %early.3 = (f32[8,4096]{1,0:T(8,128)S(1)}, f32[3,4,8,4352]{3,2,1,0:T(8,128)S(1)}, f32[8,4352]{1,0:T(8,128)S(1)}, f32[8,4352]{1,0:T(8,128)S(1)}, f32[4,8,4096]{2,1,0:T(8,128)S(1)}, /*index=5*/f32[3,8,128]{2,1,0:T(8,128)S(1)}) custom-call(f32[8,8448]{1,0:T(8,128)S(1)} %get-tuple-element.37.near, f32[8,8448]{1,0:T(8,128)S(1)} %get-tuple-element.35.mine, ...), custom_call_target="tpu_custom_call" | custom-call | flops 27852800 | bytes 2228224 | tf_op jit(solution)/shard_map/early/pallas_call | solution.py:410
  24.5 5.7 %collective-permute-start.11 = (f32[8,4096]{1,0:T(8,128)S(1)}, f32[8,4096]{1,0:T(8,128)S(1)}, u32[]{:S(2)}, u32[]{:S(2)}) collective-permute-start(f32[8,4096]{1,0:T(8,128)S(1)} %get-tuple-element.52), channel_id=1, source_target_pairs={{0,8},{4,12},{8,16},{12,20},{16,24},{20,28},{1,9},{5,13},{9,17},{1... | collective-permute-start | bytes 393224 | tf_op jit(solution)/shard_map/ppermute | solution.py:502
  30.3 4.0 %early.2 = (f32[8,4096]{1,0:T(8,128)S(1)}, f32[3,4,8,4352]{3,2,1,0:T(8,128)S(1)}, f32[8,4352]{1,0:T(8,128)S(1)}, f32[8,4352]{1,0:T(8,128)S(1)}, f32[4,8,4096]{2,1,0:T(8,128)S(1)}, /*index=5*/f32[3,8,128]{2,1,0:T(8,128)S(1)}) custom-call(f32[8,8448]{1,0:T(8,128)S(1)} %get-tuple-element.37.near, f32[8,8448]{1,0:T(8,128)S(1)} %get-tuple-element.35.mine, ...), custom_call_target="tpu_custom_call" | custom-call | flops 27852800 | bytes 2228224 | tf_op jit(solution)/shard_map/early/pallas_call | solution.py:410
  34.3 3.5 %collective-permute-start.3 = (f32[8,4096]{1,0:T(8,128)S(1)}, f32[8,4096]{1,0:T(8,128)S(1)}, u32[]{:S(2)}, u32[]{:S(2)}) collective-permute-start(f32[8,4096]{1,0:T(8,128)S(1)} %get-tuple-element.38), channel_id=1, source_target_pairs={{0,8},{4,12},{8,16},{12,20},{16,24},{20,28},{1,9},{5,13},{9,17},{1... | collective-permute-start | bytes 393224 | tf_op jit(solution)/shard_map/ppermute | solution.py:502
  37.8 0.0 collective-permute-done.11.ending
  37.8 1.0 %late.3 = (f32[8,4096]{1,0:T(8,128)S(1)}, f32[8,4096]{1,0:T(8,128)S(1)}, f32[8,4096]{1,0:T(8,128)S(1)}, f32[8,4096]{1,0:T(8,128)S(1)}, f32[8,4096]{1,0:T(8,128)S...) custom-call(f32[8,8448]{1,0:T(8,128)S(1)} %get-tuple-element.35.mine, ...), custom_call_target="tpu_custom_call" | custom-call | flops 6553600 | bytes 2097152 | tf_op jit(solution)/shard_map/late/pallas_call | solution.py:435
  38.9 0.1 collective-permute-start.12
  38.9 1.6 %collective-permute-start.13 = (f32[8,4096]{1,0:T(8,128)S(1)}, f32[8,4096]{1,0:T(8,128)S(1)}, u32[]{:S(2)}, u32[]{:S(2)}) collective-permute-start(f32[8,4096]{1,0:T(8,128)S(1)} %get-tuple-element.60), channel_id=1, source_target_pairs={{0,2},{1,3},{2,0},{3,1},{4,6},{5,7},{6,4},{7,5},{8,10},{9,11},{10,... | collective-permute-start | bytes 393224 | tf_op jit(solution)/shard_map/ppermute | solution.py:524
  40.5 0.3 collective-permute-start.14
  40.8 1.5 %collective-permute-start.15 = (f32[8,4096]{1,0:T(8,128)S(1)}, f32[8,4096]{1,0:T(8,128)S(1)}, u32[]{:S(2)}, u32[]{:S(2)}) collective-permute-start(f32[8,4096]{1,0:T(8,128)S(1)} %get-tuple-element.62), channel_id=1, source_target_pairs={{0,4},{1,5},{2,6},{3,7},{4,0},{5,1},{6,2},{7,3},{8,12},{9,13},{10,... | collective-permute-start | bytes 393224 | tf_op jit(solution)/shard_map/ppermute | solution.py:524
  42.3 0.0 collective-permute-done.3.ending
  42.3 0.2 collective-permute-start.16
  42.5 1.0 %late.2 = (f32[8,4096]{1,0:T(8,128)S(1)}, f32[8,4096]{1,0:T(8,128)S(1)}, f32[8,4096]{1,0:T(8,128)S(1)}, f32[8,4096]{1,0:T(8,128)S(1)}, f32[8,4096]{1,0:T(8,128)S...) custom-call(f32[8,8448]{1,0:T(8,128)S(1)} %get-tuple-element.35.mine, ...), custom_call_target="tpu_custom_call" | custom-call | flops 6553600 | bytes 2097152 | tf_op jit(solution)/shard_map/late/pallas_call | solution.py:435
  43.5 2.5 %collective-permute-start.17 = (f32[8,4096]{1,0:T(8,128)S(1)}, f32[8,4096]{1,0:T(8,128)S(1)}, u32[]{:S(2)}, u32[]{:S(2)}) collective-permute-start(f32[8,4096]{1,0:T(8,128)S(1)} %get-tuple-element.64), channel_id=1, source_target_pairs={{0,6},{1,7},{2,4},{3,5},{4,2},{5,3},{6,0},{7,1},{8,14},{9,15},{10,... | collective-permute-start | bytes 393224 | tf_op jit(solution)/shard_map/ppermute | solution.py:524
  46.0 0.0 collective-permute-done.13.refs_2_
  46.0 0.4 collective-permute-start.18
  46.5 0.6 collective-permute-done.14.refs_3_
  47.1 3.2 %collective-permute-start.10 = (f32[8,4096]{1,0:T(8,128)S(1)}, f32[8,4096]{1,0:T(8,128)S(1)}, u32[]{:S(2)}, u32[]{:S(2)}) collective-permute-start(f32[8,4096]{1,0:T(8,128)S(1)} %get-tuple-element.51), channel_id=1, source_target_pairs={{0,7},{1,6},{2,5},{3,4},{4,3},{5,2},{6,1},{7,0},{8,15},{9,14},{10,... | collective-permute-start | bytes 393224 | tf_op jit(solution)/shard_map/ppermute | solution.py:524
  50.4 0.0 collective-permute-done.15.refs_4_
  50.4 0.0 collective-permute-start.4
  50.4 0.1 add_reduce_fusion
  50.4 0.1 reshape.28
  50.6 8.9 %all_to_all.6 = f32[32,1,128]{2,1,0:T(1,128)S(1)} all-to-all(f32[32,1,128]{2,1,0:T(1,128)S(1)} %broadcast_in_dim.10), channel_id=1, replica_groups=mesh['tm'=8,'node'=4] {'tm','node'}, dimensions={0} | all-to-all | bytes 32768 | tf_op jit(solution)/shard_map/all_to_all | solution.py:529
  59.4 0.0 collective-permute-done.16.refs_5_
  59.5 0.6 collective-permute-start.5
  60.0 0.0 collective-permute-done.17.refs_6_
  60.0 0.7 collective-permute-start.6
  60.7 0.0 collective-permute-done.18.refs_7_
  60.7 0.5 collective-permute-start.7
  61.3 1.8 %collective-permute-start.8 = (f32[8,4096]{1,0:T(8,128)S(1)}, f32[8,4096]{1,0:T(8,128)S(1)}, u32[]{:S(2)}, u32[]{:S(2)}) collective-permute-start(f32[8,4096]{1,0:T(8,128)S(1)} %get-tuple-element.49), channel_id=1, source_target_pairs={{0,5},{1,4},{2,7},{3,6},{4,1},{5,0},{6,3},{7,2},{8,13},{9,12},{10,... | collective-permute-start | bytes 393224 | tf_op jit(solution)/shard_map/ppermute | solution.py:524
  63.0 1.0 %collective-permute-start.9 = (f32[8,4096]{1,0:T(8,128)S(1)}, f32[8,4096]{1,0:T(8,128)S(1)}, u32[]{:S(2)}, u32[]{:S(2)}) collective-permute-start(f32[8,4096]{1,0:T(8,128)S(1)} %get-tuple-element.50), channel_id=1, source_target_pairs={{0,6},{1,7},{2,4},{3,5},{4,2},{5,3},{6,0},{7,1},{8,14},{9,15},{10,... | collective-permute-start | bytes 393224 | tf_op jit(solution)/shard_map/ppermute | solution.py:524
  64.0 0.1 reshape.30
  64.1 0.7 log.11
  64.8 1.0 %assemble.2.refs_8_ = f32[32,16384]{1,0:T(8,128)} custom-call(f32[8,4096]{1,0:T(8,128)S(1)} %get-tuple-element.58.refs_0_, f32[8,4096]{1,0:T(8,128)S(1)} %collective-permute-done.12.refs_1_, f32[8,4096]{1,0:T(8,128)S(1)} %collective-permute-done.13.refs_2_, f32[8,4096]{1,0:T(8,128)S(1)} %collective-permute-done.14.refs_3_, ...), custom_call_target="tpu_custom_call" | custom-call | flops 262144 | bytes 2097152 | tf_op jit(solution)/shard_map/assemble/pallas_call | solution.py:477
  65.8 0.1 collective-permute-done.5.refs_2_
  65.9 0.6 collective-permute-done.6.refs_3_
  66.5 1.3 %collective-permute-done.7.refs_4_ = f32[8,4096]{1,0:T(8,128)S(1)} collective-permute-done((f32[8,4096]{1,0:T(8,128)S(1)}, f32[8,4096]{1,0:T(8,128)S(1)}, u32[]{:S(2)}, u32[]{:S(2)}) %collective-permute-start.7) | collective-permute-done | bytes 131104 | tf_op jit(solution)/shard_map/ppermute | solution.py:524
  67.8 4.8 %collective-permute-done.8.refs_5_ = f32[8,4096]{1,0:T(8,128)S(1)} collective-permute-done((f32[8,4096]{1,0:T(8,128)S(1)}, f32[8,4096]{1,0:T(8,128)S(1)}, u32[]{:S(2)}, u32[]{:S(2)}) %collective-permute-start.8) | collective-permute-done | bytes 131104 | tf_op jit(solution)/shard_map/ppermute | solution.py:524
  72.6 1.0 %assemble.3 = f32[32,16384]{1,0:T(8,128)} custom-call(f32[8,4096]{1,0:T(8,128)S(1)} %get-tuple-element.44.refs_0_, f32[8,4096]{1,0:T(8,128)S(1)} %collective-permute-done.4.refs_1_, f32[8,4096]{1,0:T(8,128)S(1)} %collective-permute-done.5.refs_2_, f32[8,4096]{1,0:T(8,128)S(1)} %collective-permute-done.6.refs_3_, ...), custom_call_target="tpu_custom_call", output_to_operand_aliasing={{}: (8, {})} | custom-call | flops 262144 | bytes 2097152 | tf_op jit(solution)/shard_map/assemble/pallas_call | solution.py:477
  (11 shorter events, 0.1 us)
Async XLA Ops:
  0.6 1.6 %copy-start = (f32[1,32,16384]{2,1,0:T(8,128)S(1)}, f32[1,32,16384]{2,1,0:T(8,128)}, u32[]{:S(2)}) copy-start(f32[1,32,16384]{2,1,0:T(8,128)} %param.2) | copy-start | bytes 6291460
  2.2 1.6 %copy-start.1 = (f32[32,16384]{1,0:T(8,128)S(1)}, f32[32,16384]{1,0:T(8,128)}, u32[]{:S(2)}) copy-start(f32[32,16384]{1,0:T(8,128)} %couplings.1) | copy-start | bytes 6291460
  4.0 11.8 %collective-permute-start.1 = (f32[8,8448]{1,0:T(8,128)S(1)}, f32[8,8448]{1,0:T(8,128)S(1)}, u32[]{:S(2)}, u32[]{:S(2)}) collective-permute-start(f32[8,8448]{1,0:T(8,128)S(1)} %get-tuple-element.35.mine), channel_id=1, source_target_pairs={{0,8},{4,12},{8,16},{12,20},{16,24},{20,28},{1,9},{5,13},{9,17},{1... | collective-permute-start | bytes 811016 | tf_op jit(solution)/shard_map/ppermute | solution.py:502
  9.0 8.0 %collective-permute-start = (f32[8,8448]{1,0:T(8,128)S(1)}, f32[8,8448]{1,0:T(8,128)S(1)}, u32[]{:S(2)}, u32[]{:S(2)}) collective-permute-start(f32[8,8448]{1,0:T(8,128)S(1)} %get-tuple-element.36), channel_id=1, source_target_pairs={{0,4},{4,0},{8,12},{12,8},{16,20},{20,16},{24,28},{28,24},{1,5},{5... | collective-permute-start | bytes 811016 | tf_op jit(solution)/shard_map/ppermute | solution.py:502
  10.6 10.0 %collective-permute-start.2 = (f32[8,8448]{1,0:T(8,128)S(1)}, f32[8,8448]{1,0:T(8,128)S(1)}, u32[]{:S(2)}, u32[]{:S(2)}) collective-permute-start(f32[8,8448]{1,0:T(8,128)S(1)} %get-tuple-element.36), channel_id=1, source_target_pairs={{0,12},{4,8},{8,20},{12,16},{16,28},{20,24},{1,13},{5,9},{9,21},{1... | collective-permute-start | bytes 811016 | tf_op jit(solution)/shard_map/ppermute | solution.py:502
  24.5 13.3 %collective-permute-start.11 = (f32[8,4096]{1,0:T(8,128)S(1)}, f32[8,4096]{1,0:T(8,128)S(1)}, u32[]{:S(2)}, u32[]{:S(2)}) collective-permute-start(f32[8,4096]{1,0:T(8,128)S(1)} %get-tuple-element.52), channel_id=1, source_target_pairs={{0,8},{4,12},{8,16},{12,20},{16,24},{20,28},{1,9},{5,13},{9,17},{1... | collective-permute-start | bytes 393224 | tf_op jit(solution)/shard_map/ppermute | solution.py:502
  34.3 8.0 %collective-permute-start.3 = (f32[8,4096]{1,0:T(8,128)S(1)}, f32[8,4096]{1,0:T(8,128)S(1)}, u32[]{:S(2)}, u32[]{:S(2)}) collective-permute-start(f32[8,4096]{1,0:T(8,128)S(1)} %get-tuple-element.38), channel_id=1, source_target_pairs={{0,8},{4,12},{8,16},{12,20},{16,24},{20,28},{1,9},{5,13},{9,17},{1... | collective-permute-start | bytes 393224 | tf_op jit(solution)/shard_map/ppermute | solution.py:502
  38.9 4.7 %collective-permute-start.12 = (f32[8,4096]{1,0:T(8,128)S(1)}, f32[8,4096]{1,0:T(8,128)S(1)}, u32[]{:S(2)}, u32[]{:S(2)}) collective-permute-start(f32[8,4096]{1,0:T(8,128)S(1)} %get-tuple-element.59), channel_id=1, source_target_pairs={{0,1},{1,0},{2,3},{3,2},{4,5},{5,4},{6,7},{7,6},{8,9},{9,8},{10,11... | collective-permute-start | bytes 393224 | tf_op jit(solution)/shard_map/ppermute | solution.py:524
  38.9 7.1 %collective-permute-start.13 = (f32[8,4096]{1,0:T(8,128)S(1)}, f32[8,4096]{1,0:T(8,128)S(1)}, u32[]{:S(2)}, u32[]{:S(2)}) collective-permute-start(f32[8,4096]{1,0:T(8,128)S(1)} %get-tuple-element.60), channel_id=1, source_target_pairs={{0,2},{1,3},{2,0},{3,1},{4,6},{5,7},{6,4},{7,5},{8,10},{9,11},{10,... | collective-permute-start | bytes 393224 | tf_op jit(solution)/shard_map/ppermute | solution.py:524
  40.5 6.6 %collective-permute-start.14 = (f32[8,4096]{1,0:T(8,128)S(1)}, f32[8,4096]{1,0:T(8,128)S(1)}, u32[]{:S(2)}, u32[]{:S(2)}) collective-permute-start(f32[8,4096]{1,0:T(8,128)S(1)} %get-tuple-element.61), channel_id=1, source_target_pairs={{0,3},{1,2},{2,1},{3,0},{4,7},{5,6},{6,5},{7,4},{8,11},{9,10},{10,... | collective-permute-start | bytes 393224 | tf_op jit(solution)/shard_map/ppermute | solution.py:524
  40.8 9.6 %collective-permute-start.15 = (f32[8,4096]{1,0:T(8,128)S(1)}, f32[8,4096]{1,0:T(8,128)S(1)}, u32[]{:S(2)}, u32[]{:S(2)}) collective-permute-start(f32[8,4096]{1,0:T(8,128)S(1)} %get-tuple-element.62), channel_id=1, source_target_pairs={{0,4},{1,5},{2,6},{3,7},{4,0},{5,1},{6,2},{7,3},{8,12},{9,13},{10,... | collective-permute-start | bytes 393224 | tf_op jit(solution)/shard_map/ppermute | solution.py:524
  42.3 17.1 %collective-permute-start.16 = (f32[8,4096]{1,0:T(8,128)S(1)}, f32[8,4096]{1,0:T(8,128)S(1)}, u32[]{:S(2)}, u32[]{:S(2)}) collective-permute-start(f32[8,4096]{1,0:T(8,128)S(1)} %get-tuple-element.63), channel_id=1, source_target_pairs={{0,5},{1,4},{2,7},{3,6},{4,1},{5,0},{6,3},{7,2},{8,13},{9,12},{10,... | collective-permute-start | bytes 393224 | tf_op jit(solution)/shard_map/ppermute | solution.py:524
  43.5 16.5 %collective-permute-start.17 = (f32[8,4096]{1,0:T(8,128)S(1)}, f32[8,4096]{1,0:T(8,128)S(1)}, u32[]{:S(2)}, u32[]{:S(2)}) collective-permute-start(f32[8,4096]{1,0:T(8,128)S(1)} %get-tuple-element.64), channel_id=1, source_target_pairs={{0,6},{1,7},{2,4},{3,5},{4,2},{5,3},{6,0},{7,1},{8,14},{9,15},{10,... | collective-permute-start | bytes 393224 | tf_op jit(solution)/shard_map/ppermute | solution.py:524
  46.0 14.7 %collective-permute-start.18 = (f32[8,4096]{1,0:T(8,128)S(1)}, f32[8,4096]{1,0:T(8,128)S(1)}, u32[]{:S(2)}, u32[]{:S(2)}) collective-permute-start(f32[8,4096]{1,0:T(8,128)S(1)} %get-tuple-element.65), channel_id=1, source_target_pairs={{0,7},{1,6},{2,5},{3,4},{4,3},{5,2},{6,1},{7,0},{8,15},{9,14},{10,... | collective-permute-start | bytes 393224 | tf_op jit(solution)/shard_map/ppermute | solution.py:524
  47.1 14.2 %collective-permute-start.10 = (f32[8,4096]{1,0:T(8,128)S(1)}, f32[8,4096]{1,0:T(8,128)S(1)}, u32[]{:S(2)}, u32[]{:S(2)}) collective-permute-start(f32[8,4096]{1,0:T(8,128)S(1)} %get-tuple-element.51), channel_id=1, source_target_pairs={{0,7},{1,6},{2,5},{3,4},{4,3},{5,2},{6,1},{7,0},{8,15},{9,14},{10,... | collective-permute-start | bytes 393224 | tf_op jit(solution)/shard_map/ppermute | solution.py:524
  50.4 12.7 %collective-permute-start.4 = (f32[8,4096]{1,0:T(8,128)S(1)}, f32[8,4096]{1,0:T(8,128)S(1)}, u32[]{:S(2)}, u32[]{:S(2)}) collective-permute-start(f32[8,4096]{1,0:T(8,128)S(1)} %get-tuple-element.45), channel_id=1, source_target_pairs={{0,1},{1,0},{2,3},{3,2},{4,5},{5,4},{6,7},{7,6},{8,9},{9,8},{10,11... | collective-permute-start | bytes 393224 | tf_op jit(solution)/shard_map/ppermute | solution.py:524
  59.5 6.4 %collective-permute-start.5 = (f32[8,4096]{1,0:T(8,128)S(1)}, f32[8,4096]{1,0:T(8,128)S(1)}, u32[]{:S(2)}, u32[]{:S(2)}) collective-permute-start(f32[8,4096]{1,0:T(8,128)S(1)} %get-tuple-element.46), channel_id=1, source_target_pairs={{0,2},{1,3},{2,0},{3,1},{4,6},{5,7},{6,4},{7,5},{8,10},{9,11},{10,... | collective-permute-start | bytes 393224 | tf_op jit(solution)/shard_map/ppermute | solution.py:524
  60.0 6.4 %collective-permute-start.6 = (f32[8,4096]{1,0:T(8,128)S(1)}, f32[8,4096]{1,0:T(8,128)S(1)}, u32[]{:S(2)}, u32[]{:S(2)}) collective-permute-start(f32[8,4096]{1,0:T(8,128)S(1)} %get-tuple-element.47), channel_id=1, source_target_pairs={{0,3},{1,2},{2,1},{3,0},{4,7},{5,6},{6,5},{7,4},{8,11},{9,10},{10,... | collective-permute-start | bytes 393224 | tf_op jit(solution)/shard_map/ppermute | solution.py:524
  60.7 7.1 %collective-permute-start.7 = (f32[8,4096]{1,0:T(8,128)S(1)}, f32[8,4096]{1,0:T(8,128)S(1)}, u32[]{:S(2)}, u32[]{:S(2)}) collective-permute-start(f32[8,4096]{1,0:T(8,128)S(1)} %get-tuple-element.48), channel_id=1, source_target_pairs={{0,4},{1,5},{2,6},{3,7},{4,0},{5,1},{6,2},{7,3},{8,12},{9,13},{10,... | collective-permute-start | bytes 393224 | tf_op jit(solution)/shard_map/ppermute | solution.py:524
  61.3 11.4 %collective-permute-start.8 = (f32[8,4096]{1,0:T(8,128)S(1)}, f32[8,4096]{1,0:T(8,128)S(1)}, u32[]{:S(2)}, u32[]{:S(2)}) collective-permute-start(f32[8,4096]{1,0:T(8,128)S(1)} %get-tuple-element.49), channel_id=1, source_target_pairs={{0,5},{1,4},{2,7},{3,6},{4,1},{5,0},{6,3},{7,2},{8,13},{9,12},{10,... | collective-permute-start | bytes 393224 | tf_op jit(solution)/shard_map/ppermute | solution.py:524
  63.0 9.6 %collective-permute-start.9 = (f32[8,4096]{1,0:T(8,128)S(1)}, f32[8,4096]{1,0:T(8,128)S(1)}, u32[]{:S(2)}, u32[]{:S(2)}) collective-permute-start(f32[8,4096]{1,0:T(8,128)S(1)} %get-tuple-element.50), channel_id=1, source_target_pairs={{0,6},{1,7},{2,4},{3,5},{4,2},{5,3},{6,0},{7,1},{8,14},{9,15},{10,... | collective-permute-start | bytes 393224 | tf_op jit(solution)/shard_map/ppermute | solution.py:524

commit v2 on v1

v2 whole, which is shorter than its diff:
```python
import functools

import jax
import jax.numpy as jnp
from jax import lax
from jax.experimental import pallas as pl
from jax.experimental.pallas import tpu as pltpu
from jax.sharding import PartitionSpec as P


M = 4
SWEEPS = 3
NEWTON = 2
LANES = 128
GROUP = 22
HOME_ORDER = sorted(range(1, 2 * M), key=lambda step: (step % 2, -step))
LARGE_LIMIT = 24 * 1024 * 1024
SMALL_LIMIT = 8 * 1024 * 1024

time_step = 0.5
log_floor = 0.05


def legendre_gap(point, node_count):
    before = 1.0
    current = point
    for degree in range(1, node_count):
        following = ((2 * degree + 1) * point * current - degree * before) / (degree + 1)
        before = current
        current = following
    return current - before


def collocation(node_count):
    points = []
    samples = 4000
    for sample_index in range(samples - 1):
        lower_end = -1.0 + 2.0 * sample_index / samples
        upper_end = -1.0 + 2.0 * (sample_index + 1) / samples
        lower_value = legendre_gap(lower_end, node_count)
        upper_value = legendre_gap(upper_end, node_count)
        if lower_value * upper_value < 0.0:
            for _ in range(80):
                middle = 0.5 * (lower_end + upper_end)
                middle_value = legendre_gap(middle, node_count)
                if lower_value * middle_value <= 0.0:
                    upper_end = middle
                else:
                    lower_end = middle
                    lower_value = middle_value
            points.append(0.5 * (lower_end + upper_end))
    points.append(1.0)
    node_times = [(point + 1.0) / 2.0 for point in points]
    matrix = [[0.0] * node_count for _ in range(node_count)]
    for column in range(node_count):
        coeffs = [1.0]
        for other in range(node_count):
            if other != column:
                scale = node_times[column] - node_times[other]
                shifted = [0.0] + coeffs
                scaled = [value * node_times[other] for value in coeffs] + [0.0]
                coeffs = [(shifted[power] - scaled[power]) / scale for power in range(len(shifted))]
        for row_index in range(node_count):
            upper_time = node_times[row_index]
            matrix[row_index][column] = sum(
                (
                    coeffs[power] * upper_time ** (power + 1) / (power + 1)
                    for power in range(len(coeffs))
                )
            )
    return (node_times, matrix)


NODE_TIMES, MATRIX = collocation(M)
LAST = M - 1
WEIGHTS = [[time_step * entry for entry in row] for row in MATRIX]
ROW_SUMS = [time_step * moment for moment in NODE_TIMES]
IMPLICIT = [time_step * moment / M for moment in NODE_TIMES]


def newton_steps(base, value, square, weight):
    rest = base - weight * value
    tripled = square * (3.0 * weight)
    cubic = tripled * value
    target = rest + cubic * (1.0 / 3.0)
    value = (rest + cubic) / (tripled + (1.0 - weight))
    for _ in range(1, NEWTON):
        tripled = (value * value) * (3.0 * weight)
        numerator = target + (tripled * value) * (2.0 / 3.0)
        value = numerator / (tripled + (1.0 - weight))
    return value


def weighted(terms, row):
    total = terms[0] * row[0]
    for term, entry in zip(terms[1:], row[1:]):
        total = total + term * entry
    return total


def group_of(count):
    return max(size for size in range(1, GROUP + 1) if count % size == 0)


def lanes_at(offset):
    return pl.ds(pl.multiple_of(offset, LANES), LANES)


def tracks(source, target, row, column, cells, core, sem):
    rows = target.shape[0]
    part = source.at[pl.ds(pl.multiple_of(row, rows), rows), :]
    before = pl.multiple_of(lax.rem(column + (cells - LANES), cells), LANES)
    after = pl.multiple_of(lax.rem(column + core, cells), LANES)
    middle = pl.multiple_of(column, LANES)
    return [
        pltpu.make_async_copy(
            part.at[:, pl.ds(before, LANES)], target.at[:, pl.ds(0, LANES)], sem.at[0]
        ),
        pltpu.make_async_copy(
            part.at[:, pl.ds(middle, core)], target.at[:, pl.ds(LANES, core)], sem.at[1]
        ),
        pltpu.make_async_copy(
            part.at[:, pl.ds(after, LANES)],
            target.at[:, pl.ds(LANES + core, LANES)],
            sem.at[2],
        ),
    ]


def place():
    position = lax.axis_index("tm")
    return lax.rem(position, 2), lax.div(position, 2), lax.axis_index("node")


def split_kernel(starts, couplings, mine, other, near, sems):
    side, _, node = place()
    rows, length = mine.shape
    cells = starts.shape[1]
    core = length - 2 * LANES
    copies = []
    for slot, (source, target, which) in enumerate(
        ((starts, mine, side), (starts, other, 1 - side), (couplings, near, side))
    ):
        copies += tracks(source, target, node * rows, which * core, cells, core, sems.at[slot])
    for copy in copies:
        copy.start()
    for copy in copies:
        copy.wait()


def split_starts(starts, couplings, rows, length):
    return pl.pallas_call(
        split_kernel,
        out_shape=[jax.ShapeDtypeStruct((rows, length), jnp.float32)] * 3,
        in_specs=[pl.BlockSpec(memory_space=pltpu.HBM)] * 2,
        out_specs=[pl.BlockSpec(memory_space=pltpu.VMEM)] * 3,
        scratch_shapes=[pltpu.SemaphoreType.DMA((3, 3))],
        compiler_params=pltpu.CompilerParams(vmem_limit_bytes=SMALL_LIMIT),
        cost_estimate=pl.CostEstimate(
            flops=rows * length, bytes_accessed=24 * rows * length, transcendentals=0
        ),
        name="split",
    )(*(pltpu.with_memory_space_constraint(a, pltpu.HBM) for a in (starts, couplings)))


def edge_masks(rows):
    lane = lax.broadcasted_iota(jnp.int32, (rows, LANES), 1)
    return lane, lane == 0, lane == LANES - 1


def over(rows, length, base, visits):
    count = length // LANES - 2 * base
    size = group_of(count)

    def step(group, totals):
        start = (base + group * size) * LANES
        totals = list(totals)

        def tile_at(tile):
            offset = start + tile * LANES
            if base == 0 and tile < 0:
                offset = jnp.maximum(offset, 0)
            if base == 0 and tile >= size:
                offset = jnp.minimum(offset, length - LANES)
            return lanes_at(offset)

        for tile in range(size):
            for index, visit in enumerate(visits):
                share = visit(tile_at, tile)
                if share is None:
                    continue
                if base == 0 and tile == 0:
                    share = jnp.where(group == 0, 0.0, share)
                if base == 0 and tile == size - 1:
                    share = jnp.where(group == count // size - 1, 0.0, share)
                totals[index] = totals[index] + share
        return tuple(totals)

    zero = jnp.zeros((rows, LANES), jnp.float32)
    return lax.fori_loop(0, count // size, step, (zero,) * len(visits))


def keep(ref):
    def store(index, at, value):
        ref[0, index, :, at] = value
        ref[1, index, :, at] = pltpu.roll(value, LANES - 1, 1)
        ref[2, index, :, at] = pltpu.roll(value, 1, 1)

    return store


def neighbours(masks, ahead, behind, at, above, below):
    is_first, is_last = masks
    return (
        jnp.where(is_last, ahead[:, above], ahead[:, at]),
        jnp.where(is_first, behind[:, below], behind[:, at]),
    )


def opening(pieces, masks, start, refs, store, nodes):
    coupling, left_coupling, local = pieces
    here, ahead, behind = refs

    def visit(tile_at, tile):
        at, above, below = tile_at(tile), tile_at(tile + 1), tile_at(tile - 1)
        value = here[:, at]
        right, left = neighbours(masks, ahead, behind, at, above, below)
        square = value * value
        flow = coupling[:, at] * right + left_coupling[:, at] * left
        slope = flow + value * (local[:, at] - square)
        origin = start(at)
        share = None
        for index in nodes:
            base = origin + slope * ROW_SUMS[index]
            defect = base - value
            share = defect * defect if share is None else share + defect * defect
            store(index, at, newton_steps(base, value, square, IMPLICIT[index]))
        return share

    return visit


def later(pieces, masks, start, ref, store, nodes):
    coupling, left_coupling, local = pieces

    def visit(tile_at, tile):
        at, above, below = tile_at(tile), tile_at(tile + 1), tile_at(tile - 1)
        values, squares, slopes = [], [], []
        for index in range(M):
            value = ref[0, index, :, at]
            right, left = neighbours(
                masks, ref.at[1, index], ref.at[2, index], at, above, below
            )
            square = value * value
            flow = coupling[:, at] * right + left_coupling[:, at] * left
            values.append(value)
            squares.append(square)
            slopes.append(flow + value * (local[:, at] - square))
        origin = start(at)
        share = None
        for index in nodes:
            base = origin + weighted(slopes, WEIGHTS[index])
            defect = base - values[index]
            share = defect * defect if share is None else share + defect * defect
            store(index, at, newton_steps(base, values[index], squares[index], IMPLICIT[index]))
        return share

    return visit


def inner(at):
    return pl.ds(at.start - LANES, LANES)


def emit(done):
    def store(index, at, value):
        done[index, :, inner(at)] = value

    return store


def pair_kernel(
    near, mine, partner, left_coupling, local, v_lo, v_lo_ahead, v_lo_behind, u_hi, squares,
    v_hi, v_hi_ahead, v_hi_behind,
):
    side, _, _ = place()
    even = side == 0
    rows, length = near.shape
    _, is_first, is_last = edge_masks(rows)

    def prepare(tile_at, tile):
        at, below = tile_at(tile), tile_at(tile - 1)
        own = near[:, at]
        before = jnp.where(is_first, pltpu.roll(near[:, below], 1, 1), pltpu.roll(own, 1, 1))
        left_coupling[:, at] = before
        local[:, at] = 1.0 - own - before
        for picks, here, ahead, behind in (
            ((mine, partner), v_lo, v_lo_ahead, v_lo_behind),
            ((partner, mine), v_hi, v_hi_ahead, v_hi_behind),
        ):
            value = jnp.where(even, picks[0][:, at], picks[1][:, at])
            here[:, at] = value
            ahead[:, at] = pltpu.roll(value, LANES - 1, 1)
            behind[:, at] = pltpu.roll(value, 1, 1)

    over(rows, length, 0, [prepare])
    (hi_0,) = over(
        rows,
        length,
        0,
        [
            opening(
                (near, left_coupling, local), (is_first, is_last), lambda s: v_lo[:, s],
                (v_hi, v_hi_ahead, v_hi_behind), keep(u_hi), range(M),
            )
        ],
    )
    squares[...] = hi_0


def start_kernel(
    near, straight, crossed, left_coupling, local, v_lo, v_lo_ahead, v_lo_behind, u_hi, before,
    ending, e_h1, u_lo, w_hi, squares, v_h1, v_h1_ahead, v_h1_behind,
):
    side, pair, _ = place()
    first = pair == 0
    even = side == 0
    rows, length = near.shape
    _, is_first, is_last = edge_masks(rows)
    pieces, masks = (near, left_coupling, local), (is_first, is_last)

    def prepare(tile_at, tile):
        at = tile_at(tile)
        value = jnp.where(even, crossed[:, at], straight[:, at])
        v_h1[:, at] = value
        v_h1_ahead[:, at] = pltpu.roll(value, LANES - 1, 1)
        v_h1_behind[:, at] = pltpu.roll(value, 1, 1)

    over(rows, length, 0, [prepare])

    def keep_end(index, at, value):
        e_h1[:, at] = value

    _, lo_0 = over(
        rows,
        length,
        0,
        [
            opening(
                pieces, masks,
                lambda s: jnp.where(even, straight[:, s], crossed[:, s]),
                (v_h1, v_h1_ahead, v_h1_behind), keep_end, [LAST],
            ),
            opening(
                pieces, masks,
                lambda s: jnp.where(first, v_lo[:, s], v_h1[:, s]),
                (v_lo, v_lo_ahead, v_lo_behind), keep(u_lo), range(M),
            ),
        ],
    )
    (hi_1,) = over(
        rows,
        length,
        0,
        [later(pieces, masks, lambda s: u_lo[0, LAST, :, s], u_hi, keep(w_hi), range(M))],
    )

    def finish(tile_at, tile):
        at = tile_at(tile)
        ending[:, inner(at)] = w_hi[0, LAST, :, at]

    over(rows, length, 1, [finish])
    squares[0] = before[...] + lo_0
    squares[1] = hi_1


def middle_kernel(
    near, left_coupling, local, v_lo, e_h1, u_lo, w_hi, before, w_lo, done, squares
):
    _, pair, _ = place()
    first = pair == 0
    rows, length = near.shape
    _, is_first, is_last = edge_masks(rows)
    pieces, masks = (near, left_coupling, local), (is_first, is_last)
    (lo_1,) = over(
        rows,
        length,
        0,
        [
            later(
                pieces, masks,
                lambda s: jnp.where(first, v_lo[:, s], e_h1[:, s]),
                u_lo, keep(w_lo), range(M),
            )
        ],
    )
    (hi_2,) = over(
        rows,
        length,
        1,
        [later(pieces, masks, lambda s: w_lo[0, LAST, :, s], w_hi, emit(done), range(M))],
    )
    squares[0] = before[0]
    squares[1] = before[1] + lo_1
    squares[2] = hi_2


def late_kernel(near, left_coupling, local, v_lo, ending, w_lo, done, before, *refs):
    outs, (payload, fresh) = refs[: 2 * M], refs[2 * M :]
    side, pair, node = place()
    first = pair == 0
    rows, length = near.shape
    lane, is_first, is_last = edge_masks(rows)
    (lo_2,) = over(
        rows,
        length,
        1,
        [
            later(
                (near, left_coupling, local), (is_first, is_last),
                lambda s: jnp.where(first, v_lo[:, s], ending[:, inner(s)]),
                w_lo, emit(fresh), range(M),
            )
        ],
    )

    def hand_over(lo_flip):
        def copy(tile_at, tile):
            at = inner(tile_at(tile))
            for other in range(M):
                outs[lo_flip * M + other][:, at] = fresh[other ^ node, :, at]
                outs[(1 - lo_flip) * M + other][:, at] = done[other ^ node, :, at]

        over(rows, length, 1, [copy])

    for index in range(2):

        @pl.when(side == index)
        def _(index=index):
            hand_over(index)

    system = lax.broadcasted_iota(jnp.int32, (rows, LANES), 0)
    mine = lane == node * rows + system
    shares = []
    for index in range(SWEEPS):
        total = before[index] + lo_2 if index == SWEEPS - 1 else before[index]
        column = jnp.where(mine, jnp.sum(total, axis=1, keepdims=True), 0.0)
        shares.append(jnp.sum(column, axis=0, keepdims=True))
    tile = jnp.concatenate(
        shares + [jnp.zeros((payload.shape[1] - SWEEPS, LANES), jnp.float32)], axis=0
    )
    for index in range(payload.shape[0]):
        payload[index] = tile


def call(kernel, operands, results, scratch, flops, limit):
    vmem = pl.BlockSpec(memory_space=pltpu.VMEM)
    return pl.pallas_call(
        kernel,
        out_shape=[jax.ShapeDtypeStruct(shape, jnp.float32) for shape in results],
        in_specs=[vmem] * len(operands),
        out_specs=[vmem] * len(results),
        scratch_shapes=[pltpu.VMEM(shape, jnp.float32) for shape in scratch],
        compiler_params=pltpu.CompilerParams(vmem_limit_bytes=limit),
        cost_estimate=pl.CostEstimate(flops=flops, bytes_accessed=flops, transcendentals=0),
    )(*operands)


def final_kernel(scale, count, shared, *refs):
    blocks = refs[:count]
    out, residual, save = refs[count:]
    side, _, node = place()
    rows, half = blocks[0].shape
    copies = []
    for index, block in enumerate(blocks):
        flip, other = index // M, index % M
        column = (side if flip == 0 else 1 - side) * half
        target = out.at[
            pl.ds(pl.multiple_of((other ^ node) * rows, rows), rows),
            pl.ds(pl.multiple_of(column, LANES), half),
        ]
        copies.append(pltpu.make_async_copy(block, target, save.at[index]))
    for copy in copies:
        copy.start()
    total = shared[0]
    for index in range(1, shared.shape[0]):
        total = total + shared[index]
    logs = jnp.log(log_floor + total / scale)
    residual[...] = logs[: residual.shape[0], : residual.shape[1]]
    for copy in copies:
        copy.wait()


def finish(shared, blocks, systems, scale):
    rows, half = blocks[0].shape
    count = len(blocks)
    vmem = pl.BlockSpec(memory_space=pltpu.VMEM)
    return pl.pallas_call(
        functools.partial(final_kernel, scale, count),
        out_shape=[
            jax.ShapeDtypeStruct((systems, 2 * half), jnp.float32),
            jax.ShapeDtypeStruct((SWEEPS, systems), jnp.float32),
        ],
        in_specs=[vmem] * (1 + count),
        out_specs=[pl.BlockSpec(memory_space=pltpu.HBM), vmem],
        scratch_shapes=[pltpu.SemaphoreType.DMA((count,))],
        compiler_params=pltpu.CompilerParams(vmem_limit_bytes=SMALL_LIMIT),
        cost_estimate=pl.CostEstimate(
            flops=count * rows * half, bytes_accessed=8 * count * rows * half, transcendentals=0
        ),
        name="finish",
    )(shared, *blocks)


def body(slice_starts, coupling):
    slices = lax.axis_size("tm")
    systems, cells = coupling.shape
    rows = systems // M
    half = cells // 2
    length = half + 2 * LANES
    count = slices * M
    flat, wide, core = (rows, length), (3, M, rows, length), (rows, half)
    small = (rows, LANES)

    def moved(value, target):
        pairs = [(i, target(i)) for i in range(slices)]
        return lax.ppermute(value, "tm", [(i, j) for i, j in pairs if 0 <= j < slices])

    mine, other, near = split_starts(slice_starts[0], coupling, rows, length)
    partner = moved(other, lambda i: i ^ 1)
    crossed = moved(other, lambda i: (i ^ 1) + 2)
    straight = moved(mine, lambda i: i + 2)
    left_coupling, local, *v_lo, u_hi, squares = call(
        pair_kernel, (near, mine, partner),
        [flat] * 5 + [wide, small], [flat] * 3, 200 * rows * length, LARGE_LIMIT,
    )
    ending, e_h1, u_lo, w_hi, squares = call(
        start_kernel,
        (near, straight, crossed, left_coupling, local, *v_lo, u_hi, squares),
        [core, flat, wide, wide, (2,) + small], [flat] * 3, 400 * rows * length, LARGE_LIMIT,
    )
    ending = moved(ending, lambda i: i + 2)
    w_lo, done, squares = call(
        middle_kernel,
        (near, left_coupling, local, v_lo[0], e_h1, u_lo, w_hi, squares),
        [wide, (M,) + core, (SWEEPS,) + small], [], 400 * rows * length, LARGE_LIMIT,
    )
    *outs, payload = call(
        late_kernel,
        (near, left_coupling, local, v_lo[0], ending, w_lo, done, squares),
        [core] * (2 * M) + [(count, 8, LANES)], [(M,) + core], 200 * rows * length,
        LARGE_LIMIT,
    )
    blocks = list(outs)
    for step in HOME_ORDER:
        pairs = [(i, i ^ step) for i in range(count)]
        blocks[step] = lax.ppermute(outs[step], ("tm", "node"), pairs)
    shared = lax.all_to_all(payload, ("tm", "node"), 0, 0)
    result, residual_log = finish(shared, blocks, systems, slices * M * cells)
    return (result[None, None], residual_log)


def solution(mesh):
    placed = (P("tm", None, None), P())

    return jax.shard_map(
        body,
        mesh=mesh,
        in_specs=placed,
        out_specs=(P("tm", "node", None, None), P()),
        check_vma=False,
    )
```

time: 73.9 us -> 65 us (0.88)
  starting transfers between devices: 33.5 us -> 21.5 us
  blocking collectives: 8.87 us -> 18.3 us
  local copies, waits for them, and re-layouts: 4.04 us -> 0 us
  waiting for transfers between devices: 14 us -> 10.6 us
  Pallas kernels: 12.3 us -> 13.6 us
    all_to_all x1, blocking collectives: 8.87 us -> 18.3 us  [body(): shared = lax.all_to_all(payload, ('tm', 'node'), 0, 0)]
    ppermute x14 -> x7, starting transfers between devices: 14.3 us -> 7.16 us  [body(): blocks[step] = lax.ppermute(outs[step], ('tm', 'node'), pairs)]
    ppermute x5 -> x4, starting transfers between devices: 19.2 us -> 14.3 us  [moved(): lax.ppermute(value, 'tm', [(i, j) for i, j in pairs if 0 <= j < slices])]
    ppermute x14 -> x7, waiting for transfers between devices: 7.49 us -> 3.25 us  [body(): blocks[step] = lax.ppermute(outs[step], ('tm', 'node'), pairs)]
    unnamed x4 -> x0, local copies, waits for them, and re-layouts: 3.17 us -> none
    pallas_call x1, Pallas kernels: 0.18 us -> 1.29 us  [split_starts(): pl.pallas_call(split_kernel, out_shape=[jax.ShapeDtypeStruct((rows, lengt...]
    ppermute x5 -> x4, waiting for transfers between devices: 6.54 us -> 7.38 us  [moved(): lax.ppermute(value, 'tm', [(i, j) for i, j in pairs if 0 <= j < slices])]
    log x3 -> x0, local copies, waits for them, and re-layouts: 0.76 us -> none  [body(): residual_log = jnp.log(log_floor + summed / (slices * M * cells))]
  transfers between devices with their start and end apart: 19 -> 11, of which waited for: 8 -> 4; matrix products, arithmetic and copies ran while one was open for 1% -> 0% of each run, Pallas kernels for 10% -> 7%
where the time goes in v2:
time: 65 us; the launch traced here: 64.7 us
  starting transfers between devices  21.5 us (33%)
  blocking collectives  18.3 us (28%)
  Pallas kernels  13.6 us (21%)
  waiting for transfers between devices  10.6 us (16%)
  between operations  0.72 us (1%)
    all_to_all x1, blocking collectives, body(): shared = lax.all_to_all(payload, ('tm', 'node'), 0, 0)  18.3 us
    ppermute x4, starting transfers between devices, moved(): lax.ppermute(value, 'tm', [(i, j) for i, j in pairs if 0 <= j < slices])  14.3 us
    pallas_call x4, Pallas kernels, call(): pl.pallas_call(kernel, out_shape=[jax.ShapeDtypeStruct(shape, jnp.float32...  10.3 us
    ppermute x4, waiting for transfers between devices, moved(): lax.ppermute(value, 'tm', [(i, j) for i, j in pairs if 0 <= j < slices])  7.38 us
    ppermute x7, starting transfers between devices, body(): blocks[step] = lax.ppermute(outs[step], ('tm', 'node'), pairs)  7.16 us
    ppermute x7, waiting for transfers between devices, body(): blocks[step] = lax.ppermute(outs[step], ('tm', 'node'), pairs)  3.25 us
    pallas_call x1, Pallas kernels, finish(): pl.pallas_call(functools.partial(final_kernel, scale, count), out_shape=[...  1.97 us
  transfers between devices with their start and end apart: 11, of which 4 were waited for; matrix products, arithmetic and copies ran while one was open for 0% of the time, Pallas kernels for 7%

profile of v2, /device:TPU:0, one launch (start us, length us, event | category | flops | bytes accessed | tf_op | source)
XLA Modules:
  0.0 64.7 jit_solution(7386642718906120464)
XLA Ops:
  0.6 1.3 %split.1 = (f32[8,8448]{1,0:T(8,128)S(1)}, f32[8,8448]{1,0:T(8,128)S(1)}, f32[8,8448]{1,0:T(8,128)S(1)}) custom-call(f32[32,16384]{1,0:T(8,128)} %bitcast.2, f32[32,16384]{1,0:T(8,128)} %couplings.1), custom_call_target="tpu_custom_call" | custom-call | flops 67584 | bytes 1622016 | tf_op jit(solution)/shard_map/split/pallas_call | solution.py:152
  1.9 3.1 %collective-permute-start = (f32[8,8448]{1,0:T(8,128)S(1)}, f32[8,8448]{1,0:T(8,128)S(1)}, u32[]{:S(2)}, u32[]{:S(2)}) collective-permute-start(f32[8,8448]{1,0:T(8,128)S(1)} %get-tuple-element.33), channel_id=1, source_target_pairs={{0,4},{4,0},{8,12},{12,8},{16,20},{20,16},{24,28},{28,24},{1,5},{5... | collective-permute-start | bytes 811016 | tf_op jit(solution)/shard_map/ppermute | solution.py:527
  5.0 3.5 %collective-permute-start.1 = (f32[8,8448]{1,0:T(8,128)S(1)}, f32[8,8448]{1,0:T(8,128)S(1)}, u32[]{:S(2)}, u32[]{:S(2)}) collective-permute-start(f32[8,8448]{1,0:T(8,128)S(1)} %get-tuple-element.32.mine), channel_id=1, source_target_pairs={{0,8},{4,12},{8,16},{12,20},{16,24},{20,28},{1,9},{5,13},{9,17},{1... | collective-permute-start | bytes 811016 | tf_op jit(solution)/shard_map/ppermute | solution.py:527
  8.5 3.4 %collective-permute-start.2 = (f32[8,8448]{1,0:T(8,128)S(1)}, f32[8,8448]{1,0:T(8,128)S(1)}, u32[]{:S(2)}, u32[]{:S(2)}) collective-permute-start(f32[8,8448]{1,0:T(8,128)S(1)} %get-tuple-element.33), channel_id=1, source_target_pairs={{0,12},{4,8},{8,20},{12,16},{16,28},{20,24},{1,13},{5,9},{9,21},{1... | collective-permute-start | bytes 811016 | tf_op jit(solution)/shard_map/ppermute | solution.py:527
  11.9 0.0 collective-permute-done.partner
  11.9 1.8 %shard_map.41 = (f32[8,8448]{1,0:T(8,128)S(1)}, f32[8,8448]{1,0:T(8,128)S(1)}, f32[8,8448]{1,0:T(8,128)S(1)}, f32[8,8448]{1,0:T(8,128)S(1)}, f32[8,8448]{1,0:T(8...) custom-call(f32[8,8448]{1,0:T(8,128)S(1)} %get-tuple-element.31.near, ...), custom_call_target="tpu_custom_call" | custom-call | flops 13516800 | bytes 13516800 | tf_op jit(solution)/shard_map/pallas_call | solution.py:458
  13.7 1.6 %collective-permute-done.1.straight = f32[8,8448]{1,0:T(8,128)S(1)} collective-permute-done((f32[8,8448]{1,0:T(8,128)S(1)}, f32[8,8448]{1,0:T(8,128)S(1)}, u32[]{:S(2)}, u32[]{:S(2)}) %collective-permute-start.1) | collective-permute-done | bytes 270368 | tf_op jit(solution)/shard_map/ppermute | solution.py:527
  15.3 4.4 %collective-permute-done.2.crossed = f32[8,8448]{1,0:T(8,128)S(1)} collective-permute-done((f32[8,8448]{1,0:T(8,128)S(1)}, f32[8,8448]{1,0:T(8,128)S(1)}, u32[]{:S(2)}, u32[]{:S(2)}) %collective-permute-start.2) | collective-permute-done | bytes 270368 | tf_op jit(solution)/shard_map/ppermute | solution.py:527
  19.7 3.5 %shard_map.42 = (f32[8,8192]{1,0:T(8,128)S(1)}, f32[8,8448]{1,0:T(8,128)S(1)}, f32[3,4,8,8448]{3,2,1,0:T(8,128)S(1)}, f32[3,4,8,8448]{3,2,1,0:T(8,128)S(1)}, f32[2,8,128]{2,1,0:T(8,128)S(1)}) custom-call(f32[8,8448]{1,0:T(8,128)S(1)} %get-tuple-element.31.near, f32[8,8448]{1,0:T(8,128)S(1)} %collective-permute-done.1.straight, ...), custom_call_target="tpu_custom_call" | custom-call | flops 27033600 | bytes 27033600 | tf_op jit(solution)/shard_map/pallas_call | solution.py:458
  23.2 4.3 %collective-permute-start.3 = (f32[8,8192]{1,0:T(8,128)S(1)}, f32[8,8192]{1,0:T(8,128)S(1)}, u32[]{:S(2)}, u32[]{:S(2)}) collective-permute-start(f32[8,8192]{1,0:T(8,128)S(1)} %get-tuple-element.41), channel_id=1, source_target_pairs={{0,8},{4,12},{8,16},{12,20},{16,24},{20,28},{1,9},{5,13},{9,17},{1... | collective-permute-start | bytes 786440 | tf_op jit(solution)/shard_map/ppermute | solution.py:527
  27.6 3.0 %shard_map.43 = (f32[3,4,8,8448]{3,2,1,0:T(8,128)S(1)}, f32[4,8,8192]{2,1,0:T(8,128)S(1)}, f32[3,8,128]{2,1,0:T(8,128)S(1)}) custom-call(f32[8,8448]{1,0:T(8,128)S(1)} %get-tuple-element.31.near, f32[8,8448]{1,0:T(8,128)S(1)} %get-tuple-element.34.left_coupling, f32[8,8448]{1,0:T(8,128)S(1)} %get-tuple-element.35.local, ...), custom_call_target="tpu_custom_call" | custom-call | flops 27033600 | bytes 27033600 | tf_op jit(solution)/shard_map/pallas_call | solution.py:458
  30.6 1.4 %collective-permute-done.3.ending = f32[8,8192]{1,0:T(8,128)S(1)} collective-permute-done((f32[8,8192]{1,0:T(8,128)S(1)}, f32[8,8192]{1,0:T(8,128)S(1)}, u32[]{:S(2)}, u32[]{:S(2)}) %collective-permute-start.3) | collective-permute-done | bytes 262176 | tf_op jit(solution)/shard_map/ppermute | solution.py:527
  32.0 2.0 %shard_map.44 = (f32[8,8192]{1,0:T(8,128)S(1)}, f32[8,8192]{1,0:T(8,128)S(1)}, f32[8,8192]{1,0:T(8,128)S(1)}, f32[8,8192]{1,0:T(8,128)S(1)}, f32[8,8192]{1,0:T(8...) custom-call(f32[8,8448]{1,0:T(8,128)S(1)} %get-tuple-element.31.near, ...), custom_call_target="tpu_custom_call" | custom-call | flops 13516800 | bytes 13516800 | tf_op jit(solution)/shard_map/pallas_call | solution.py:458
  34.0 0.1 collective-permute-start.4
  34.1 1.6 %collective-permute-start.5 = (f32[8,8192]{1,0:T(8,128)S(1)}, f32[8,8192]{1,0:T(8,128)S(1)}, u32[]{:S(2)}, u32[]{:S(2)}) collective-permute-start(f32[8,8192]{1,0:T(8,128)S(1)} %get-tuple-element.52), channel_id=1, source_target_pairs={{0,2},{1,3},{2,0},{3,1},{4,6},{5,7},{6,4},{7,5},{8,10},{9,11},{10,... | collective-permute-start | bytes 786440 | tf_op jit(solution)/shard_map/ppermute | solution.py:557
  35.6 0.3 collective-permute-start.6
  35.9 1.5 %collective-permute-start.7 = (f32[8,8192]{1,0:T(8,128)S(1)}, f32[8,8192]{1,0:T(8,128)S(1)}, u32[]{:S(2)}, u32[]{:S(2)}) collective-permute-start(f32[8,8192]{1,0:T(8,128)S(1)} %get-tuple-element.54), channel_id=1, source_target_pairs={{0,4},{1,5},{2,6},{3,7},{4,0},{5,1},{6,2},{7,3},{8,12},{9,13},{10,... | collective-permute-start | bytes 786440 | tf_op jit(solution)/shard_map/ppermute | solution.py:557
  37.4 0.2 collective-permute-start.8
  37.6 0.0 collective-permute-done.4.refs_1_
  37.6 2.4 %collective-permute-start.9 = (f32[8,8192]{1,0:T(8,128)S(1)}, f32[8,8192]{1,0:T(8,128)S(1)}, u32[]{:S(2)}, u32[]{:S(2)}) collective-permute-start(f32[8,8192]{1,0:T(8,128)S(1)} %get-tuple-element.56), channel_id=1, source_target_pairs={{0,6},{1,7},{2,4},{3,5},{4,2},{5,3},{6,0},{7,1},{8,14},{9,15},{10,... | collective-permute-start | bytes 786440 | tf_op jit(solution)/shard_map/ppermute | solution.py:557
  40.1 3.2 %collective-permute-done.5.refs_2_ = f32[8,8192]{1,0:T(8,128)S(1)} collective-permute-done((f32[8,8192]{1,0:T(8,128)S(1)}, f32[8,8192]{1,0:T(8,128)S(1)}, u32[]{:S(2)}, u32[]{:S(2)}) %collective-permute-start.5) | collective-permute-done | bytes 262176 | tf_op jit(solution)/shard_map/ppermute | solution.py:557
  43.3 1.1 %collective-permute-start.10 = (f32[8,8192]{1,0:T(8,128)S(1)}, f32[8,8192]{1,0:T(8,128)S(1)}, u32[]{:S(2)}, u32[]{:S(2)}) collective-permute-start(f32[8,8192]{1,0:T(8,128)S(1)} %get-tuple-element.57), channel_id=1, source_target_pairs={{0,7},{1,6},{2,5},{3,4},{4,3},{5,2},{6,1},{7,0},{8,15},{9,14},{10,... | collective-permute-start | bytes 786440 | tf_op jit(solution)/shard_map/ppermute | solution.py:557
  44.4 18.3 %all_to_all.5.shared = f32[32,8,128]{2,1,0:T(8,128)S(1)} all-to-all(f32[32,8,128]{2,1,0:T(8,128)S(1)} %get-tuple-element.49), channel_id=1, replica_groups=mesh['tm'=8,'node'=4] {'tm','node'}, dimensions={0} | all-to-all | bytes 262144 | tf_op jit(solution)/shard_map/all_to_all | solution.py:558
  62.7 0.0 collective-permute-done.6.refs_3_
  62.7 0.0 collective-permute-done.7.refs_4_
  62.7 0.0 collective-permute-done.8.refs_5_
  62.8 0.0 collective-permute-done.9.refs_6_
  62.8 0.0 collective-permute-done.10.refs_7_
  62.8 2.0 %finish.1 = (f32[32,16384]{1,0:T(8,128)}, f32[3,32]{1,0:T(4,128)}) custom-call(f32[32,8,128]{2,1,0:T(8,128)S(1)} %all_to_all.5.shared, f32[8,8192]{1,0:T(8,128)S(1)} %get-tuple-element.50.refs_0_, f32[8,8192]{1,0:T(8,128)S(1)} %collective-permute-done.4.refs_1_, f32[8,8192]{1,0:T(8,128)S(1)} %collective-permute-done.5.refs_2_, ...), custom_call_target="tpu_custom_call" | custom-call | flops 524288 | bytes 4194304 | tf_op jit(solution)/shard_map/finish/pallas_call | solution.py:498
Async XLA Ops:
  1.9 10.0 %collective-permute-start = (f32[8,8448]{1,0:T(8,128)S(1)}, f32[8,8448]{1,0:T(8,128)S(1)}, u32[]{:S(2)}, u32[]{:S(2)}) collective-permute-start(f32[8,8448]{1,0:T(8,128)S(1)} %get-tuple-element.33), channel_id=1, source_target_pairs={{0,4},{4,0},{8,12},{12,8},{16,20},{20,16},{24,28},{28,24},{1,5},{5... | collective-permute-start | bytes 811016 | tf_op jit(solution)/shard_map/ppermute | solution.py:527
  5.0 10.3 %collective-permute-start.1 = (f32[8,8448]{1,0:T(8,128)S(1)}, f32[8,8448]{1,0:T(8,128)S(1)}, u32[]{:S(2)}, u32[]{:S(2)}) collective-permute-start(f32[8,8448]{1,0:T(8,128)S(1)} %get-tuple-element.32.mine), channel_id=1, source_target_pairs={{0,8},{4,12},{8,16},{12,20},{16,24},{20,28},{1,9},{5,13},{9,17},{1... | collective-permute-start | bytes 811016 | tf_op jit(solution)/shard_map/ppermute | solution.py:527
  8.5 11.2 %collective-permute-start.2 = (f32[8,8448]{1,0:T(8,128)S(1)}, f32[8,8448]{1,0:T(8,128)S(1)}, u32[]{:S(2)}, u32[]{:S(2)}) collective-permute-start(f32[8,8448]{1,0:T(8,128)S(1)} %get-tuple-element.33), channel_id=1, source_target_pairs={{0,12},{4,8},{8,20},{12,16},{16,28},{20,24},{1,13},{5,9},{9,21},{1... | collective-permute-start | bytes 811016 | tf_op jit(solution)/shard_map/ppermute | solution.py:527
  23.2 8.7 %collective-permute-start.3 = (f32[8,8192]{1,0:T(8,128)S(1)}, f32[8,8192]{1,0:T(8,128)S(1)}, u32[]{:S(2)}, u32[]{:S(2)}) collective-permute-start(f32[8,8192]{1,0:T(8,128)S(1)} %get-tuple-element.41), channel_id=1, source_target_pairs={{0,8},{4,12},{8,16},{12,20},{16,24},{20,28},{1,9},{5,13},{9,17},{1... | collective-permute-start | bytes 786440 | tf_op jit(solution)/shard_map/ppermute | solution.py:527
  34.0 3.6 %collective-permute-start.4 = (f32[8,8192]{1,0:T(8,128)S(1)}, f32[8,8192]{1,0:T(8,128)S(1)}, u32[]{:S(2)}, u32[]{:S(2)}) collective-permute-start(f32[8,8192]{1,0:T(8,128)S(1)} %get-tuple-element.51), channel_id=1, source_target_pairs={{0,1},{1,0},{2,3},{3,2},{4,5},{5,4},{6,7},{7,6},{8,9},{9,8},{10,11... | collective-permute-start | bytes 786440 | tf_op jit(solution)/shard_map/ppermute | solution.py:557
  34.1 9.2 %collective-permute-start.5 = (f32[8,8192]{1,0:T(8,128)S(1)}, f32[8,8192]{1,0:T(8,128)S(1)}, u32[]{:S(2)}, u32[]{:S(2)}) collective-permute-start(f32[8,8192]{1,0:T(8,128)S(1)} %get-tuple-element.52), channel_id=1, source_target_pairs={{0,2},{1,3},{2,0},{3,1},{4,6},{5,7},{6,4},{7,5},{8,10},{9,11},{10,... | collective-permute-start | bytes 786440 | tf_op jit(solution)/shard_map/ppermute | solution.py:557
  35.6 27.1 %collective-permute-start.6 = (f32[8,8192]{1,0:T(8,128)S(1)}, f32[8,8192]{1,0:T(8,128)S(1)}, u32[]{:S(2)}, u32[]{:S(2)}) collective-permute-start(f32[8,8192]{1,0:T(8,128)S(1)} %get-tuple-element.53), channel_id=1, source_target_pairs={{0,3},{1,2},{2,1},{3,0},{4,7},{5,6},{6,5},{7,4},{8,11},{9,10},{10,... | collective-permute-start | bytes 786440 | tf_op jit(solution)/shard_map/ppermute | solution.py:557
  35.9 26.8 %collective-permute-start.7 = (f32[8,8192]{1,0:T(8,128)S(1)}, f32[8,8192]{1,0:T(8,128)S(1)}, u32[]{:S(2)}, u32[]{:S(2)}) collective-permute-start(f32[8,8192]{1,0:T(8,128)S(1)} %get-tuple-element.54), channel_id=1, source_target_pairs={{0,4},{1,5},{2,6},{3,7},{4,0},{5,1},{6,2},{7,3},{8,12},{9,13},{10,... | collective-permute-start | bytes 786440 | tf_op jit(solution)/shard_map/ppermute | solution.py:557
  37.4 25.3 %collective-permute-start.8 = (f32[8,8192]{1,0:T(8,128)S(1)}, f32[8,8192]{1,0:T(8,128)S(1)}, u32[]{:S(2)}, u32[]{:S(2)}) collective-permute-start(f32[8,8192]{1,0:T(8,128)S(1)} %get-tuple-element.55), channel_id=1, source_target_pairs={{0,5},{1,4},{2,7},{3,6},{4,1},{5,0},{6,3},{7,2},{8,13},{9,12},{10,... | collective-permute-start | bytes 786440 | tf_op jit(solution)/shard_map/ppermute | solution.py:557
  37.6 25.1 %collective-permute-start.9 = (f32[8,8192]{1,0:T(8,128)S(1)}, f32[8,8192]{1,0:T(8,128)S(1)}, u32[]{:S(2)}, u32[]{:S(2)}) collective-permute-start(f32[8,8192]{1,0:T(8,128)S(1)} %get-tuple-element.56), channel_id=1, source_target_pairs={{0,6},{1,7},{2,4},{3,5},{4,2},{5,3},{6,0},{7,1},{8,14},{9,15},{10,... | collective-permute-start | bytes 786440 | tf_op jit(solution)/shard_map/ppermute | solution.py:557
  43.3 19.5 %collective-permute-start.10 = (f32[8,8192]{1,0:T(8,128)S(1)}, f32[8,8192]{1,0:T(8,128)S(1)}, u32[]{:S(2)}, u32[]{:S(2)}) collective-permute-start(f32[8,8192]{1,0:T(8,128)S(1)} %get-tuple-element.57), channel_id=1, source_target_pairs={{0,7},{1,6},{2,5},{3,4},{4,3},{5,2},{6,1},{7,0},{8,15},{9,14},{10,... | collective-permute-start | bytes 786440 | tf_op jit(solution)/shard_map/ppermute | solution.py:557
